TPU v7x, 512 devices: a whole 4x4x16 slice. The times are simulated.
512 devices in a mesh: row: 64 (over y, z_lo, x), col: 8 (over z_hi, core).
Axes of the slice: x: 4, y: 4, z: 16 (z_hi: 4, z_lo: 4; z = z_hi * 4 + z_lo), core: 2. Of those that a mesh axis runs over, the one named last changes fastest.
Arguments:
- environment: float32 [6144, 6144], P('row', 'col'), may hold values from -6 to 6
- site_tensors: float32 [2, 6144, 6144], P(None, 'row', 'col'), may hold values from -0.078125 to 0.078125
- panel_offset: int32 [1], replicated, may hold values from 0 to 6016
Outputs:
- new_panel: float32 [128, 6144], P('row', 'col')
All inputs are finite; a program needn't handle non-finite values.
Results may differ from a plain program's by a relative error of at most 0.0001.
Values sent between devices are 32-bit elements; how exact they have to be, the bound alone decides.
No kernel may reach another device: no remote copies, remote signals or barrier semaphores. Data moves between devices by JAX's collectives and lax.ppermute only.
A program may use at most 64 MiB of HBM per device.

v0:
```python
import jax
import jax.numpy as jnp
from jax import lax
from jax.sharding import PartitionSpec as P

PHYS = 2
PANEL = 128


def total_of_pieces(shard, axis):
    pieces = lax.all_gather(shard, axis)
    return pieces.sum(axis=0)


def in_blocks(shard, dim, peers):
    dims = shard.shape
    pieces = shard.reshape(*dims[:dim], peers, dims[dim] // peers, *dims[dim + 1 :])
    return jnp.moveaxis(pieces, dim, 0)


def sum_at_owner(shard, axis, dim):
    peers = lax.axis_size(axis)
    pieces = lax.all_to_all(in_blocks(shard, dim, peers), axis, 0, 0, tiled=True)
    return jnp.sum(pieces, axis=0)


def from_everyone(shard, axis):
    peers = lax.axis_size(axis)
    return lax.all_to_all(
        jnp.broadcast_to(shard[None], (peers, *shard.shape)), axis, 0, 0, tiled=True
    )


def of_everyone(shard, axis):
    return from_everyone(shard, axis).sum(axis=0)


def shards(environment, site_tensors, panel_offset):
    rows_local = environment.shape[0]
    cols_local = environment.shape[1]
    col_index = lax.axis_index("col")
    row_index = lax.axis_index("row")
    row_count = lax.axis_size("row")
    col_count = lax.axis_size("col")
    group_rows = row_count // col_count
    padded = jnp.pad(site_tensors, ((0, 0), (0, 0), (PANEL, PANEL)))
    slice_start = jnp.clip(panel_offset[0] - col_index * cols_local + PANEL, 0, cols_local + PANEL)
    window = lax.dynamic_slice_in_dim(padded, slice_start, PANEL, 2)
    panel_rows = total_of_pieces(window, "col")
    first_col = row_index * rows_local
    owner_col = first_col // cols_local
    owner_mask = (col_index == owner_col).astype(jnp.float32)
    accumulated = jnp.zeros((PANEL, cols_local), jnp.float32)
    partial_all = jnp.einsum(
        "sip,ij->spj", panel_rows, environment, precision=lax.Precision.HIGHEST
    )
    count_s = partial_all.shape[0]
    shares = sum_at_owner(partial_all, "row", 1)
    share_rows = shares.shape[1]
    pieces = shares.reshape(count_s, share_rows, group_rows, rows_local).transpose(2, 0, 1, 3)
    slots = jnp.zeros((row_count, count_s, share_rows, rows_local), jnp.float32)
    slots = lax.dynamic_update_slice_in_dim(slots, pieces, col_index * group_rows, 0)
    received = lax.all_to_all(slots, "row", split_axis=0, concat_axis=2, tiled=True)
    block_all = received[0]
    fetched = of_everyone(block_all * owner_mask, "col")
    for phys in range(PHYS):
        accumulated = accumulated + jnp.dot(
            fetched[phys],
            site_tensors[phys],
            precision=lax.Precision.HIGHEST,
            preferred_element_type=jnp.float32,
        )
    return sum_at_owner(accumulated, "row", 0)


def solution(mesh):
    return jax.shard_map(
        shards,
        mesh=mesh,
        in_specs=(P("row", "col"), P(None, "row", "col"), P()),
        out_specs=P("row", "col"),
        check_vma=False,
    )
```

profile of v0, /device:TPU:1, one launch (start us, length us, event | category | flops | bytes accessed | tf_op | source)
XLA Modules:
  0.0 156.6 jit_solution(4374034422240526370)
XLA Ops:
  0.0 0.0 copy-start
  0.7 1.0 pad_dynamic-slice_fusion
  1.7 32.7 %all-gather = f32[16,96,128]{2,1,0:T(8,128)S(1)} all-gather(f32[2,96,128]{2,1,0:T(8,128)S(1)} %pad_dynamic-slice_fusion), channel_id=2, replica_groups=mesh['row'=64,'col'=8] {'col'}, dimensions={0}, use_global_device_ids=true | all-gather | bytes 884736 | tf_op jit(solution)/shard_map/all_gather | solution.py:11
  34.4 0.1 copy.12
  34.5 0.0 copy-done
  34.6 0.8 convolution_bitcast_fusion
  35.3 1.5 copy.14
  36.8 8.8 %all-to-all-start = ((f32[64,2,2,768]{3,2,1,0:T(2,128)}), f32[64,2,2,768]{3,2,1,0:T(2,128)S(1)}, u32[]{:S(2)}, u32[]{:S(2)}) async-start(f32[64,2,2,768]{3,2,1,0:T(2,128)} %copy.14), calls=%async_computation | async-start | bytes 1572864 | tf_op jit(solution)/shard_map/all_to_all | solution.py:23
  45.7 22.9 %all-to-all-done = f32[64,2,2,768]{3,2,1,0:T(2,128)S(1)} async-done(((f32[64,2,2,768]{3,2,1,0:T(2,128)}), f32[64,2,2,768]{3,2,1,0:T(2,128)S(1)}, u32[]{:S(2)}, u32[]{:S(2)}) %all-to-all-start) | async-done | bytes 786464 | tf_op jit(solution)/shard_map/all_to_all | solution.py:23
  68.6 0.3 reduce_sum.37
  68.8 0.1 reshape.18
  68.9 0.7 broadcast_in_dim.4
  69.6 0.6 copy_dynamic-update-slice_fusion
  70.2 5.6 %all-to-all-start.1 = ((f32[64,2,2,96]{3,2,1,0:T(2,128)}), f32[64,2,2,96]{3,2,1,0:T(2,128)S(1)}, u32[]{:S(2)}, u32[]{:S(2)}) async-start(f32[64,2,2,96]{3,2,1,0:T(2,128)} %copy_dynamic-update-slice_fusion), calls=%async_computation.1 | async-start | bytes 262144 | tf_op jit(solution)/shard_map/all_to_all | solution.py:63
  75.8 9.5 %all-to-all-done.1 = f32[64,2,2,96]{3,2,1,0:T(2,128)S(1)} async-done(((f32[64,2,2,96]{3,2,1,0:T(2,128)}), f32[64,2,2,96]{3,2,1,0:T(2,128)S(1)}, u32[]{:S(2)}, u32[]{:S(2)}) %all-to-all-start.1) | async-done | bytes 98336 | tf_op jit(solution)/shard_map/all_to_all | solution.py:63
  85.4 0.1 copy.17
  85.5 0.1 broadcast_in_dim.10
  85.6 47.3 %all_to_all.24 = f32[8,2,128,96]{2,3,1,0:T(8,128)S(1)} all-to-all(f32[8,2,128,96]{2,3,1,0:T(8,128)S(1)} %broadcast_in_dim.10), channel_id=1, replica_groups=mesh['row'=64,'col'=8] {'col'}, dimensions={0} | all-to-all | bytes 1572864 | tf_op jit(solution)/shard_map/all_to_all | solution.py:29
  132.9 0.0 copy-start.1
  132.9 1.0 copy-done.1
  133.9 0.5 fusion.2
  134.5 0.5 convolution_add_fusion
  135.0 0.2 reshape.19
  135.2 20.6 %all_to_all.25 = f32[64,2,768]{2,1,0:T(2,128)S(1)} all-to-all(f32[64,2,768]{2,1,0:T(2,128)S(1)} %reshape.19), channel_id=1, replica_groups=mesh['row'=64,'col'=8] {'row'}, dimensions={0} | all-to-all | bytes 786432 | tf_op jit(solution)/shard_map/all_to_all | solution.py:23
  155.9 0.7 reduce_sum.39
  (4 shorter events, 0.2 us)
Async XLA Ops:
  0.0 34.5 %copy-start = (f32[96,768]{1,0:T(8,128)S(1)}, f32[96,768]{1,0:T(8,128)}, u32[]{:S(2)}) copy-start(f32[96,768]{1,0:T(8,128)} %param.3) | copy-start | bytes 884740
  36.8 31.8 %all-to-all-start = ((f32[64,2,2,768]{3,2,1,0:T(2,128)}), f32[64,2,2,768]{3,2,1,0:T(2,128)S(1)}, u32[]{:S(2)}, u32[]{:S(2)}) async-start(f32[64,2,2,768]{3,2,1,0:T(2,128)} %copy.14), calls=%async_computation | async-start | bytes 1572864 | tf_op jit(solution)/shard_map/all_to_all | solution.py:23
  70.2 15.1 %all-to-all-start.1 = ((f32[64,2,2,96]{3,2,1,0:T(2,128)}), f32[64,2,2,96]{3,2,1,0:T(2,128)S(1)}, u32[]{:S(2)}, u32[]{:S(2)}) async-start(f32[64,2,2,96]{3,2,1,0:T(2,128)} %copy_dynamic-update-slice_fusion), calls=%async_computation.1 | async-start | bytes 262144 | tf_op jit(solution)/shard_map/all_to_all | solution.py:63
  132.9 1.1 copy-start.1
where the time goes:
time: 159 us; the launch traced here: 157 us
  blocking collectives  101 us (64%)
  waiting for transfers between devices  32.4 us (20%)
  starting transfers between devices  14.4 us (9%)
  local copies, waits for them, and re-layouts  5.42 us (3%)
  matrix products  1.82 us (1%)
    all_to_all x1, blocking collectives, from_everyone(): lax.all_to_all(jnp.broadcast_to(shard[None], (peers, *shard.shape)), axis...  47.3 us
    all_gather x1, blocking collectives, total_of_pieces(): pieces = lax.all_gather(shard, axis)  32.7 us
    all_to_all x1, waiting for transfers between devices, sum_at_owner(): lax.all_to_all(in_blocks(shard, dim, peers), axis, 0, 0, tiled=True)  22.9 us
    all_to_all x1, blocking collectives, sum_at_owner(): lax.all_to_all(in_blocks(shard, dim, peers), axis, 0, 0, tiled=True)  20.6 us
    all_to_all x1, waiting for transfers between devices, shards(): lax.all_to_all(slots, 'row', split_axis=0, concat_axis=2, tiled=True)  9.51 us
    all_to_all x1, starting transfers between devices, sum_at_owner(): lax.all_to_all(in_blocks(shard, dim, peers), axis, 0, 0, tiled=True)  8.84 us
    all_to_all x1, starting transfers between devices, shards(): lax.all_to_all(slots, 'row', split_axis=0, concat_axis=2, tiled=True)  5.59 us
  transfers between devices with their start and end apart: 2, of which 2 were waited for; matrix products, arithmetic and copies ran while one was open for 0% of the time, Pallas kernels for 0%

commit v1 on v0

v1 whole, which is shorter than its diff:
```python
import jax
import jax.numpy as jnp
from jax import lax
from jax.sharding import Mesh, PartitionSpec as P

PHYS = 2
PANEL = 128
ROW = ("y", "zl", "x")
COL = ("zh", "core")
ALL = ROW + COL
SIZES = (4, 4, 4, 4, 2)
HOP = (3, 0, 2, 1)


def flat(y, zl, x, zh, core):
    return (((y * 4 + zl) * 4 + x) * 4 + zh) * 2 + core


def deliveries():
    pairs = []
    for y in range(4):
        s, b = y // 2, y % 2
        for zl in range(4):
            for x in range(4):
                for zh in range(4):
                    for core in range(2):
                        there = flat(zh, 2 * core + b, x, (zh + HOP[zl]) % 4, s)
                        pairs.append((flat(y, zl, x, zh, core), there))
    return pairs


def shards(environment, site_tensors, panel_offset):
    rows = environment.shape[0]
    cols = environment.shape[1]
    col_index = lax.axis_index(COL)
    core = lax.axis_index("core")
    padded = jnp.pad(site_tensors, ((0, 0), (0, 0), (PANEL, PANEL)))
    start = jnp.clip(panel_offset[0] - col_index * cols + PANEL, 0, cols + PANEL)
    window = lax.dynamic_slice_in_dim(padded, start, PANEL, 2)
    panel = lax.all_gather(window, COL).sum(axis=0)
    partial = jnp.einsum("ij,sip->sjp", environment, panel, precision=lax.Precision.HIGHEST)
    pieces = partial.reshape(16, rows, PANEL)
    pieces = lax.all_to_all(pieces, ("y", "x"), 0, 0, tiled=True)
    piece = pieces.sum(axis=0)
    piece = lax.all_gather(piece, "zl").sum(axis=0)
    mine = lax.ppermute(piece, ALL, deliveries())
    other = lax.ppermute(mine, "core", [(0, 1), (1, 0)])

    def times(block, phys):
        tensor = lax.dynamic_index_in_dim(site_tensors, phys, 0, keepdims=False)
        return jnp.einsum("jp,jm->pm", block, tensor, precision=lax.Precision.HIGHEST)

    total = times(mine, core) + times(other, 1 - core)
    shares = lax.all_to_all(total.reshape(64, 2, cols), ROW, 0, 0, tiled=True)
    return shares.sum(axis=0)


def solution(mesh):
    fine = Mesh(mesh.devices.reshape(SIZES), ALL)
    return jax.shard_map(
        shards,
        mesh=fine,
        in_specs=(P(ROW, COL), P(None, ROW, COL), P()),
        out_specs=P(ROW, COL),
        check_vma=False,
    )
```

time: 159 us -> 110 us (0.69)
  waiting for transfers between devices: 32.4 us -> 1.47 us
  blocking collectives: 101 us -> 92.1 us
  local copies, waits for them, and re-layouts: 5.42 us -> 0.59 us
  starting transfers between devices: 14.4 us -> 11.5 us
    all_to_all x2 -> x0, waiting for transfers between devices: 32.4 us -> none  [the longest x1 22.9 us: sum_at_owner(): lax.all_to_all(in_blocks(shard, dim, peers), axis, 0, 0, tiled=True)]
    all_to_all x2, blocking collectives: 67.9 us -> 48.2 us  [the longest x1 27.7 us: shards(): shares = lax.all_to_all(total.reshape(64, 2, cols), ROW, 0, 0, tiled=True)]
    all_to_all x2 -> x0, starting transfers between devices: 14.4 us -> none  [the longest x1 8.84 us: sum_at_owner(): lax.all_to_all(in_blocks(shard, dim, peers), axis, 0, 0, tiled=True)]
    ppermute x0 -> x2, starting transfers between devices: none -> 11.5 us  [the longest x1 6.89 us: shards(): mine = lax.ppermute(piece, ALL, deliveries())]
    all_gather x1 -> x2, blocking collectives: 32.7 us -> 43.9 us  [the longest x1 32.3 us: shards(): panel = lax.all_gather(window, COL).sum(axis=0)]
where the time goes in v1:
time: 110 us; the launch traced here: 109 us
  blocking collectives  92.1 us (84%)
  starting transfers between devices  11.5 us (10%)
  matrix products  1.87 us (2%)
  waiting for transfers between devices  1.47 us (1%)
    all_gather x1, blocking collectives, shards(): panel = lax.all_gather(window, COL).sum(axis=0)  32.3 us
    all_to_all x1, blocking collectives, shards(): shares = lax.all_to_all(total.reshape(64, 2, cols), ROW, 0, 0, tiled=True)  27.7 us
    all_to_all x1, blocking collectives, shards(): pieces = lax.all_to_all(pieces, ('y', 'x'), 0, 0, tiled=True)  20.6 us
    all_gather x1, blocking collectives, shards(): piece = lax.all_gather(piece, 'zl').sum(axis=0)  11.5 us
    ppermute x1, starting transfers between devices, shards(): mine = lax.ppermute(piece, ALL, deliveries())  6.89 us
    ppermute x1, starting transfers between devices, shards(): other = lax.ppermute(mine, 'core', [(0, 1), (1, 0)])  4.6 us
  transfers between devices with their start and end apart: 2, of which 2 were waited for; matrix products, arithmetic and copies ran while one was open for 0% of the time, Pallas kernels for 0%

profile of v1, /device:TPU:1, one launch (start us, length us, event | category | flops | bytes accessed | tf_op | source)
XLA Modules:
  0.0 109.2 jit_solution(10413259288063796472)
XLA Ops:
  0.0 0.0 copy-start
  0.7 0.1 pad_dynamic-slice_fusion
  0.8 32.3 %all-gather = f32[16,96,128]{2,1,0:T(8,128)S(1)} all-gather(f32[2,96,128]{2,1,0:T(8,128)S(1)} %pad_dynamic-slice_fusion), channel_id=2, replica_groups=mesh['y'=4,'zl'=4,'x'=4,'zh'=4,'core'=2] {'zh','core'}, dimensions={0}, use_global_device_ids=true | all-gather | bytes 884736 | tf_op jit(solution)/shard_map/all_gather | solution.py:40
  33.2 0.0 copy-done
  33.2 0.8 convolution_bitcast_fusion
  34.0 0.3 copy.6
  34.3 20.6 %all_to_all.10 = f32[16,96,128]{2,1,0:T(8,128)S(1)} all-to-all(f32[16,96,128]{2,1,0:T(8,128)S(1)} %bitcast.20), channel_id=1, replica_groups=mesh['y'=4,'zl'=4,'x'=4,'zh'=4,'core'=2] {'y','x'}, dimensions={0} | all-to-all | bytes 1572864 | tf_op jit(solution)/shard_map/all_to_all | solution.py:43
  54.9 0.0 copy-start.1
  54.9 11.5 %all-gather.1 = f32[384,128]{1,0:T(8,128)S(1)} all-gather(f32[96,128]{1,0:T(8,128)S(1)} %reduce_sum.37), channel_id=3, replica_groups=mesh['y'=4,'zl'=4,'x'=4,'zh'=4,'core'=2] {'zl'}, dimensions={0}, use_global_device_ids=true | all-gather | bytes 245760 | tf_op jit(solution)/shard_map/all_gather | solution.py:45
  66.5 6.9 %collective-permute-start = (f32[96,128]{1,0:T(8,128)S(1)}, f32[96,128]{1,0:T(8,128)S(1)}, u32[]{:S(2)}, u32[]{:S(2)}) collective-permute-start(f32[96,128]{1,0:T(8,128)S(1)} %reduce_sum.38), channel_id=1, source_target_pairs={{0,6},{1,70},{2,128},{3,192},{4,258},{5,322},{6,388},{7,452},{8,14... | collective-permute-start | bytes 147464 | tf_op jit(solution)/shard_map/ppermute | solution.py:46
  73.4 1.2 %collective-permute-done = f32[96,128]{1,0:T(8,128)S(1)} collective-permute-done((f32[96,128]{1,0:T(8,128)S(1)}, f32[96,128]{1,0:T(8,128)S(1)}, u32[]{:S(2)}, u32[]{:S(2)}) %collective-permute-start) | collective-permute-done | bytes 49184 | tf_op jit(solution)/shard_map/ppermute | solution.py:46
  74.5 4.6 %collective-permute-start.1 = (f32[96,128]{1,0:T(8,128)S(1)}, f32[96,128]{1,0:T(8,128)S(1)}, u32[]{:S(2)}, u32[]{:S(2)}) collective-permute-start(f32[96,128]{1,0:T(8,128)S(1)} %collective-permute-done), channel_id=1, source_target_pairs={{0,1},{1,0},{2,3},{3,2},{4,5},{5,4},{6,7},{7,6},{8,9},{9,8},{10,11... | collective-permute-start | bytes 147464 | tf_op jit(solution)/shard_map/ppermute | solution.py:47
  79.1 0.0 copy-done.1
  79.1 0.5 fusion.1
  79.7 0.3 collective-permute-done.1
  80.0 0.5 convolution_add_fusion
  80.5 0.2 reshape.7
  80.7 27.7 %all_to_all.11 = f32[64,2,768]{2,1,0:T(2,128)S(1)} all-to-all(f32[64,2,768]{2,1,0:T(2,128)S(1)} %reshape.7), channel_id=1, replica_groups=mesh['y'=4,'zl'=4,'x'=4,'zh'=4,'core'=2] {'y','zl','x'}, dimensions={0} | all-to-all | bytes 786432 | tf_op jit(solution)/shard_map/all_to_all | solution.py:54
  108.4 0.7 reduce_sum.39
  (3 shorter events, 0.1 us)
Async XLA Ops:
  0.0 33.2 %copy-start = (f32[96,768]{1,0:T(8,128)S(1)}, f32[96,768]{1,0:T(8,128)}, u32[]{:S(2)}) copy-start(f32[96,768]{1,0:T(8,128)} %param.3) | copy-start | bytes 884740
  54.9 24.3 %copy-start.1 = (f32[2,96,768]{2,1,0:T(8,128)S(1)}, f32[2,96,768]{2,1,0:T(8,128)}, u32[]{:S(2)}) copy-start(f32[2,96,768]{2,1,0:T(8,128)} %param.4) | copy-start | bytes 1769476
  66.5 8.1 %collective-permute-start = (f32[96,128]{1,0:T(8,128)S(1)}, f32[96,128]{1,0:T(8,128)S(1)}, u32[]{:S(2)}, u32[]{:S(2)}) collective-permute-start(f32[96,128]{1,0:T(8,128)S(1)} %reduce_sum.38), channel_id=1, source_target_pairs={{0,6},{1,70},{2,128},{3,192},{4,258},{5,322},{6,388},{7,452},{8,14... | collective-permute-start | bytes 147464 | tf_op jit(solution)/shard_map/ppermute | solution.py:46
  74.5 5.5 %collective-permute-start.1 = (f32[96,128]{1,0:T(8,128)S(1)}, f32[96,128]{1,0:T(8,128)S(1)}, u32[]{:S(2)}, u32[]{:S(2)}) collective-permute-start(f32[96,128]{1,0:T(8,128)S(1)} %collective-permute-done), channel_id=1, source_target_pairs={{0,1},{1,0},{2,3},{3,2},{4,5},{5,4},{6,7},{7,6},{8,9},{9,8},{10,11... | collective-permute-start | bytes 147464 | tf_op jit(solution)/shard_map/ppermute | solution.py:47

commit v2 on v1

--- a/solution.py
+++ b/solution.py
@@ -9,7 +9,7 @@
 COL = ("zh", "core")
 ALL = ROW + COL
 SIZES = (4, 4, 4, 4, 2)
-HOP = (3, 0, 2, 1)
+HOPS = ((3, 0, 1, 2), (3, 0, 1, 2), (2, 3, 0, 1), (2, 3, 0, 1))
 
 
 def flat(y, zl, x, zh, core):
@@ -24,7 +24,8 @@
             for x in range(4):
                 for zh in range(4):
                     for core in range(2):
-                        there = flat(zh, 2 * core + b, x, (zh + HOP[zl]) % 4, s)
+                        to = 2 * core + b
+                        there = flat(zh, to, x, (zh + HOPS[to][zl]) % 4, s)
                         pairs.append((flat(y, zl, x, zh, core), there))
     return pairs
 
@@ -42,7 +43,8 @@
     pieces = partial.reshape(16, rows, PANEL)
     pieces = lax.all_to_all(pieces, ("y", "x"), 0, 0, tiled=True)
     piece = pieces.sum(axis=0)
-    piece = lax.all_gather(piece, "zl").sum(axis=0)
+    copies = jnp.broadcast_to(piece[None], (4, rows, PANEL))
+    piece = lax.all_to_all(copies, "zl", 0, 0, tiled=True).sum(axis=0)
     mine = lax.ppermute(piece, ALL, deliveries())
     other = lax.ppermute(mine, "core", [(0, 1), (1, 0)])
 

time: 110 us -> 104 us (0.945)
  blocking collectives: 92.1 us -> 87.2 us
    all_gather x1 -> x0, blocking collectives: 11.5 us -> none  [shards(): piece = lax.all_gather(piece, 'zl').sum(axis=0)]
    all_to_all x0 -> x1, blocking collectives: none -> 8.5 us  [shards(): piece = lax.all_to_all(copies, 'zl', 0, 0, tiled=True).sum(axis=0)]
    ppermute x1, starting transfers between devices: 4.6 us -> 2.69 us  [shards(): other = lax.ppermute(mine, 'core', [(0, 1), (1, 0)])]
    all_to_all x1, blocking collectives: 27.7 us -> 25.9 us  [shards(): shares = lax.all_to_all(total.reshape(64, 2, cols), ROW, 0, 0, tiled=True)]
    ppermute x1, starting transfers between devices: 6.89 us -> 8.01 us  [shards(): mine = lax.ppermute(piece, ALL, deliveries())]
  transfers between devices with their start and end apart: 2 -> 2, of which waited for: 2 -> 2; matrix products, arithmetic and copies ran while one was open for 0% -> 1% of each run, Pallas kernels for 0% -> 0%
where the time goes in v2:
time: 104 us; the launch traced here: 103 us
  blocking collectives  87.2 us (84%)
  starting transfers between devices  10.7 us (10%)
  matrix products  1.88 us (2%)
  waiting for transfers between devices  1.47 us (1%)
    all_gather x1, blocking collectives, shards(): panel = lax.all_gather(window, COL).sum(axis=0)  32.2 us
    all_to_all x1, blocking collectives, shards(): shares = lax.all_to_all(total.reshape(64, 2, cols), ROW, 0, 0, tiled=True)  25.9 us
    all_to_all x1, blocking collectives, shards(): pieces = lax.all_to_all(pieces, ('y', 'x'), 0, 0, tiled=True)  20.6 us
    all_to_all x1, blocking collectives, shards(): piece = lax.all_to_all(copies, 'zl', 0, 0, tiled=True).sum(axis=0)  8.5 us
    ppermute x1, starting transfers between devices, shards(): mine = lax.ppermute(piece, ALL, deliveries())  8.01 us
    ppermute x1, starting transfers between devices, shards(): other = lax.ppermute(mine, 'core', [(0, 1), (1, 0)])  2.69 us
  transfers between devices with their start and end apart: 2, of which 2 were waited for; matrix products, arithmetic and copies ran while one was open for 1% of the time, Pallas kernels for 0%

profile of v2, /device:TPU:1, one launch (start us, length us, event | category | flops | bytes accessed | tf_op | source)
XLA Modules:
  0.0 103.5 jit_solution(13019646038072131160)
XLA Ops:
  0.0 0.0 copy-start
  0.7 0.1 pad_dynamic-slice_fusion
  0.8 32.2 %all-gather = f32[16,96,128]{2,1,0:T(8,128)S(1)} all-gather(f32[2,96,128]{2,1,0:T(8,128)S(1)} %pad_dynamic-slice_fusion), channel_id=2, replica_groups=mesh['y'=4,'zl'=4,'x'=4,'zh'=4,'core'=2] {'zh','core'}, dimensions={0}, use_global_device_ids=true | all-gather | bytes 884736 | tf_op jit(solution)/shard_map/all_gather | solution.py:41
  33.1 0.0 copy-done
  33.1 0.8 convolution_bitcast_fusion
  33.9 0.3 copy.6
  34.2 20.6 %all_to_all.15 = f32[16,96,128]{2,1,0:T(8,128)S(1)} all-to-all(f32[16,96,128]{2,1,0:T(8,128)S(1)} %bitcast.19), channel_id=1, replica_groups=mesh['y'=4,'zl'=4,'x'=4,'zh'=4,'core'=2] {'y','x'}, dimensions={0} | all-to-all | bytes 1572864 | tf_op jit(solution)/shard_map/all_to_all | solution.py:44
  54.8 0.0 copy-start.1
  54.8 8.5 %all_to_all.16 = f32[4,96,128]{2,1,0:T(8,128)S(1)} all-to-all(f32[4,96,128]{2,1,0:T(8,128)S(1)} %broadcast_in_dim.2), channel_id=1, replica_groups=mesh['y'=4,'zl'=4,'x'=4,'zh'=4,'core'=2] {'zl'}, dimensions={0} | all-to-all | bytes 393216 | tf_op jit(solution)/shard_map/all_to_all | solution.py:47
  63.4 8.0 %collective-permute-start = (f32[96,128]{1,0:T(8,128)S(1)}, f32[96,128]{1,0:T(8,128)S(1)}, u32[]{:S(2)}, u32[]{:S(2)}) collective-permute-start(f32[96,128]{1,0:T(8,128)S(1)} %reduce_sum.38), channel_id=1, source_target_pairs={{0,6},{1,68},{2,128},{3,198},{4,258},{5,320},{6,388},{7,450},{8,14... | collective-permute-start | bytes 147464 | tf_op jit(solution)/shard_map/ppermute | solution.py:48
  71.4 1.2 %collective-permute-done = f32[96,128]{1,0:T(8,128)S(1)} collective-permute-done((f32[96,128]{1,0:T(8,128)S(1)}, f32[96,128]{1,0:T(8,128)S(1)}, u32[]{:S(2)}, u32[]{:S(2)}) %collective-permute-start) | collective-permute-done | bytes 49184 | tf_op jit(solution)/shard_map/ppermute | solution.py:48
  72.5 2.7 %collective-permute-start.1 = (f32[96,128]{1,0:T(8,128)S(1)}, f32[96,128]{1,0:T(8,128)S(1)}, u32[]{:S(2)}, u32[]{:S(2)}) collective-permute-start(f32[96,128]{1,0:T(8,128)S(1)} %collective-permute-done), channel_id=1, source_target_pairs={{0,1},{1,0},{2,3},{3,2},{4,5},{5,4},{6,7},{7,6},{8,9},{9,8},{10,11... | collective-permute-start | bytes 147464 | tf_op jit(solution)/shard_map/ppermute | solution.py:49
  75.2 0.0 copy-done.1
  75.3 0.5 fusion.1
  75.8 0.3 collective-permute-done.1
  76.1 0.5 convolution_add_fusion
  76.6 0.2 reshape.8
  76.9 25.9 %all_to_all.17 = f32[64,2,768]{2,1,0:T(2,128)S(1)} all-to-all(f32[64,2,768]{2,1,0:T(2,128)S(1)} %reshape.8), channel_id=1, replica_groups=mesh['y'=4,'zl'=4,'x'=4,'zh'=4,'core'=2] {'y','zl','x'}, dimensions={0} | all-to-all | bytes 786432 | tf_op jit(solution)/shard_map/all_to_all | solution.py:56
  102.7 0.7 reduce_sum.39
  (4 shorter events, 0.1 us)
Async XLA Ops:
  0.0 33.1 %copy-start = (f32[96,768]{1,0:T(8,128)S(1)}, f32[96,768]{1,0:T(8,128)}, u32[]{:S(2)}) copy-start(f32[96,768]{1,0:T(8,128)} %param.3) | copy-start | bytes 884740
  54.8 20.4 %copy-start.1 = (f32[2,96,768]{2,1,0:T(8,128)S(1)}, f32[2,96,768]{2,1,0:T(8,128)}, u32[]{:S(2)}) copy-start(f32[2,96,768]{2,1,0:T(8,128)} %param.4) | copy-start | bytes 1769476
  63.4 9.2 %collective-permute-start = (f32[96,128]{1,0:T(8,128)S(1)}, f32[96,128]{1,0:T(8,128)S(1)}, u32[]{:S(2)}, u32[]{:S(2)}) collective-permute-start(f32[96,128]{1,0:T(8,128)S(1)} %reduce_sum.38), channel_id=1, source_target_pairs={{0,6},{1,68},{2,128},{3,198},{4,258},{5,320},{6,388},{7,450},{8,14... | collective-permute-start | bytes 147464 | tf_op jit(solution)/shard_map/ppermute | solution.py:48
  72.5 3.6 %collective-permute-start.1 = (f32[96,128]{1,0:T(8,128)S(1)}, f32[96,128]{1,0:T(8,128)S(1)}, u32[]{:S(2)}, u32[]{:S(2)}) collective-permute-start(f32[96,128]{1,0:T(8,128)S(1)} %collective-permute-done), channel_id=1, source_target_pairs={{0,1},{1,0},{2,3},{3,2},{4,5},{5,4},{6,7},{7,6},{8,9},{9,8},{10,11... | collective-permute-start | bytes 147464 | tf_op jit(solution)/shard_map/ppermute | solution.py:49

commit v3 on v2

--- a/solution.py
+++ b/solution.py
@@ -19,15 +19,19 @@
 def deliveries():
     pairs = []
     for y in range(4):
-        s, b = y // 2, y % 2
+        far, b = y // 2, y % 2
         for zl in range(4):
             for x in range(4):
                 for zh in range(4):
                     for core in range(2):
-                        to = 2 * core + b
-                        there = flat(zh, to, x, (zh + HOPS[to][zl]) % 4, s)
+                        to = 2 * (core ^ far) + b
+                        there = flat(zh, to, x, (zh + HOPS[to][zl]) % 4, core)
                         pairs.append((flat(y, zl, x, zh, core), there))
     return pairs
+
+
+def swap(values):
+    return lax.ppermute(values, "core", [(0, 1), (1, 0)])
 
 
 def shards(environment, site_tensors, panel_offset):
@@ -37,16 +41,27 @@
     core = lax.axis_index("core")
     padded = jnp.pad(site_tensors, ((0, 0), (0, 0), (PANEL, PANEL)))
     start = jnp.clip(panel_offset[0] - col_index * cols + PANEL, 0, cols + PANEL)
-    window = lax.dynamic_slice_in_dim(padded, start, PANEL, 2)
-    panel = lax.all_gather(window, COL).sum(axis=0)
-    partial = jnp.einsum("ij,sip->sjp", environment, panel, precision=lax.Precision.HIGHEST)
-    pieces = partial.reshape(16, rows, PANEL)
+    zero = jnp.zeros_like(start)
+
+    def window(phys):
+        return lax.dynamic_slice(padded, (phys, zero, start), (1, rows, PANEL))[0]
+
+    sent = jnp.concatenate([window(1 - core), environment], axis=1)
+    came = swap(sent)
+    half = window(core) + came[:, :PANEL]
+    panel = lax.all_gather(half, "zh").sum(axis=0)
+
+    def bond(block):
+        return jnp.einsum("ij,ip->jp", block, panel, precision=lax.Precision.HIGHEST)
+
+    pieces = jnp.concatenate([bond(environment), bond(came[:, PANEL:])], axis=0)
+    pieces = pieces.reshape(16, rows, PANEL)
     pieces = lax.all_to_all(pieces, ("y", "x"), 0, 0, tiled=True)
     piece = pieces.sum(axis=0)
     copies = jnp.broadcast_to(piece[None], (4, rows, PANEL))
     piece = lax.all_to_all(copies, "zl", 0, 0, tiled=True).sum(axis=0)
     mine = lax.ppermute(piece, ALL, deliveries())
-    other = lax.ppermute(mine, "core", [(0, 1), (1, 0)])
+    other = swap(mine)
 
     def times(block, phys):
         tensor = lax.dynamic_index_in_dim(site_tensors, phys, 0, keepdims=False)

time: 104 us -> 101 us (0.971)
  blocking collectives: 87.2 us -> 69.6 us
  starting transfers between devices: 10.7 us -> 22 us
  waiting for transfers between devices: 1.47 us -> 3.45 us
    all_gather x1, blocking collectives: 32.2 us -> 18.1 us  [shards(): panel = lax.all_gather(half, 'zh').sum(axis=0)]
    ppermute x1 -> x2, starting transfers between devices: 2.69 us -> 16.6 us  [swap(): return lax.ppermute(values, 'core', [(0, 1), (1, 0)])]
    all_to_all x1, blocking collectives: 20.6 us -> 17 us  [shards(): pieces = lax.all_to_all(pieces, ('y', 'x'), 0, 0, tiled=True)]
    ppermute x1, starting transfers between devices: 8.01 us -> 5.37 us  [shards(): mine = lax.ppermute(piece, ALL, deliveries())]
    ppermute x1 -> x2, waiting for transfers between devices: 0.32 us -> 1.58 us  [swap(): return lax.ppermute(values, 'core', [(0, 1), (1, 0)])]
  transfers between devices with their start and end apart: 2 -> 3, of which waited for: 2 -> 3; matrix products, arithmetic and copies ran while one was open for 1% -> 1% of each run, Pallas kernels for 0% -> 0%
where the time goes in v3:
time: 101 us; the launch traced here: 100 us
  blocking collectives  69.6 us (69%)
  starting transfers between devices  22 us (22%)
  waiting for transfers between devices  3.45 us (3%)
  matrix products  2.07 us (2%)
  local copies, waits for them, and re-layouts  1.47 us (1%)
    all_to_all x1, blocking collectives, shards(): shares = lax.all_to_all(total.reshape(64, 2, cols), ROW, 0, 0, tiled=True)  26.2 us
    all_gather x1, blocking collectives, shards(): panel = lax.all_gather(half, 'zh').sum(axis=0)  18.1 us
    all_to_all x1, blocking collectives, shards(): pieces = lax.all_to_all(pieces, ('y', 'x'), 0, 0, tiled=True)  17 us
    ppermute x2, starting transfers between devices, swap(): return lax.ppermute(values, 'core', [(0, 1), (1, 0)])  16.6 us
    all_to_all x1, blocking collectives, shards(): piece = lax.all_to_all(copies, 'zl', 0, 0, tiled=True).sum(axis=0)  8.37 us
    ppermute x1, starting transfers between devices, shards(): mine = lax.ppermute(piece, ALL, deliveries())  5.37 us
  transfers between devices with their start and end apart: 3, of which 3 were waited for; matrix products, arithmetic and copies ran while one was open for 1% of the time, Pallas kernels for 0%

profile of v3, /device:TPU:1, one launch (start us, length us, event | category | flops | bytes accessed | tf_op | source)
XLA Modules:
  0.0 100.4 jit_solution(9404136912550959233)
XLA Ops:
  0.7 0.0 copy-start.1
  0.7 0.0 copy-start
  0.7 1.0 fusion.7
  1.6 0.0 copy-done.1
  1.7 8.7 %collective-permute-start = (f32[96,896]{1,0:T(8,128)S(1)}, f32[96,896]{1,0:T(8,128)S(1)}, u32[]{:S(2)}, u32[]{:S(2)}) collective-permute-start(f32[96,896]{1,0:T(8,128)S(1)} %pad_maximum_fusion.1), channel_id=1, source_target_pairs={{0,1},{1,0},{2,3},{3,2},{4,5},{5,4},{6,7},{7,6},{8,9},{9,8},{10,11... | collective-permute-start | bytes 1032200 | tf_op jit(solution)/shard_map/ppermute | solution.py:34
  10.4 1.3 %collective-permute-done = f32[96,896]{1,0:T(8,128)S(1)} collective-permute-done((f32[96,896]{1,0:T(8,128)S(1)}, f32[96,896]{1,0:T(8,128)S(1)}, u32[]{:S(2)}, u32[]{:S(2)}) %collective-permute-start) | collective-permute-done | bytes 344096 | tf_op jit(solution)/shard_map/ppermute | solution.py:34
  11.7 0.0 copy-done
  11.7 0.1 slice_add_fusion
  11.7 18.1 %all-gather = f32[384,128]{1,0:T(8,128)S(1)} all-gather(f32[96,128]{1,0:T(8,128)S(1)} %slice_add_fusion), channel_id=2, replica_groups=mesh['y'=4,'zl'=4,'x'=4,'zh'=4,'core'=2] {'zh'}, dimensions={0}, use_global_device_ids=true | all-gather | bytes 245760 | tf_op jit(solution)/shard_map/all_gather | solution.py:52
  29.8 0.5 convolution_bitcast_fusion
  30.3 0.5 fusion
  30.9 0.1 pad_maximum_fusion
  30.9 0.3 copy.8
  31.2 17.0 %all_to_all.15 = f32[16,96,128]{2,1,0:T(8,128)S(1)} all-to-all(f32[16,96,128]{2,1,0:T(8,128)S(1)} %bitcast.21), channel_id=1, replica_groups=mesh['y'=4,'zl'=4,'x'=4,'zh'=4,'core'=2] {'y','x'}, dimensions={0} | all-to-all | bytes 1572864 | tf_op jit(solution)/shard_map/all_to_all | solution.py:59
  48.3 8.4 %all_to_all.16 = f32[4,96,128]{2,1,0:T(8,128)S(1)} all-to-all(f32[4,96,128]{2,1,0:T(8,128)S(1)} %broadcast_in_dim.2), channel_id=1, replica_groups=mesh['y'=4,'zl'=4,'x'=4,'zh'=4,'core'=2] {'zl'}, dimensions={0} | all-to-all | bytes 393216 | tf_op jit(solution)/shard_map/all_to_all | solution.py:62
  56.6 5.4 %collective-permute-start.1 = (f32[96,128]{1,0:T(8,128)S(1)}, f32[96,128]{1,0:T(8,128)S(1)}, u32[]{:S(2)}, u32[]{:S(2)}) collective-permute-start(f32[96,128]{1,0:T(8,128)S(1)} %reduce_sum.38), channel_id=1, source_target_pairs={{0,6},{1,69},{2,128},{3,199},{4,258},{5,321},{6,388},{7,451},{8,14... | collective-permute-start | bytes 147464 | tf_op jit(solution)/shard_map/ppermute | solution.py:63
  62.0 1.9 %collective-permute-done.1 = f32[96,128]{1,0:T(8,128)S(1)} collective-permute-done((f32[96,128]{1,0:T(8,128)S(1)}, f32[96,128]{1,0:T(8,128)S(1)}, u32[]{:S(2)}, u32[]{:S(2)}) %collective-permute-start.1) | collective-permute-done | bytes 49184 | tf_op jit(solution)/shard_map/ppermute | solution.py:63
  63.9 7.9 %collective-permute-start.2 = (f32[96,128]{1,0:T(8,128)S(1)}, f32[96,128]{1,0:T(8,128)S(1)}, u32[]{:S(2)}, u32[]{:S(2)}) collective-permute-start(f32[96,128]{1,0:T(8,128)S(1)} %collective-permute-done.1), channel_id=1, source_target_pairs={{0,1},{1,0},{2,3},{3,2},{4,5},{5,4},{6,7},{7,6},{8,9},{9,8},{10,11... | collective-permute-start | bytes 147464 | tf_op jit(solution)/shard_map/ppermute | solution.py:34
  71.8 0.5 fusion.3
  72.3 0.3 collective-permute-done.2
  72.7 0.5 convolution_add_fusion
  73.2 0.2 reshape.8
  73.4 26.2 %all_to_all.17 = f32[64,2,768]{2,1,0:T(2,128)S(1)} all-to-all(f32[64,2,768]{2,1,0:T(2,128)S(1)} %reshape.8), channel_id=1, replica_groups=mesh['y'=4,'zl'=4,'x'=4,'zh'=4,'core'=2] {'y','zl','x'}, dimensions={0} | all-to-all | bytes 786432 | tf_op jit(solution)/shard_map/all_to_all | solution.py:71
  99.6 0.7 reduce_sum.39
  (5 shorter events, 0.1 us)
Async XLA Ops:
  0.7 1.0 copy-start.1
  0.7 11.0 %copy-start = (f32[2,96,768]{2,1,0:T(8,128)S(1)}, f32[2,96,768]{2,1,0:T(8,128)}, u32[]{:S(2)}) copy-start(f32[2,96,768]{2,1,0:T(8,128)} %param.4) | copy-start | bytes 1769476
  1.7 10.0 %collective-permute-start = (f32[96,896]{1,0:T(8,128)S(1)}, f32[96,896]{1,0:T(8,128)S(1)}, u32[]{:S(2)}, u32[]{:S(2)}) collective-permute-start(f32[96,896]{1,0:T(8,128)S(1)} %pad_maximum_fusion.1), channel_id=1, source_target_pairs={{0,1},{1,0},{2,3},{3,2},{4,5},{5,4},{6,7},{7,6},{8,9},{9,8},{10,11... | collective-permute-start | bytes 1032200 | tf_op jit(solution)/shard_map/ppermute | solution.py:34
  56.6 7.2 %collective-permute-start.1 = (f32[96,128]{1,0:T(8,128)S(1)}, f32[96,128]{1,0:T(8,128)S(1)}, u32[]{:S(2)}, u32[]{:S(2)}) collective-permute-start(f32[96,128]{1,0:T(8,128)S(1)} %reduce_sum.38), channel_id=1, source_target_pairs={{0,6},{1,69},{2,128},{3,199},{4,258},{5,321},{6,388},{7,451},{8,14... | collective-permute-start | bytes 147464 | tf_op jit(solution)/shard_map/ppermute | solution.py:63
  63.9 8.8 %collective-permute-start.2 = (f32[96,128]{1,0:T(8,128)S(1)}, f32[96,128]{1,0:T(8,128)S(1)}, u32[]{:S(2)}, u32[]{:S(2)}) collective-permute-start(f32[96,128]{1,0:T(8,128)S(1)} %collective-permute-done.1), channel_id=1, source_target_pairs={{0,1},{1,0},{2,3},{3,2},{4,5},{5,4},{6,7},{7,6},{8,9},{9,8},{10,11... | collective-permute-start | bytes 147464 | tf_op jit(solution)/shard_map/ppermute | solution.py:34

commit v4 on v3

--- a/solution.py
+++ b/solution.py
@@ -34,6 +34,34 @@
     return lax.ppermute(values, "core", [(0, 1), (1, 0)])
 
 
+ROUTES = (((2, 1, 3), None), ((0, 2), (2, 3)), ((0, 1, 3), None), ((1, 0, 2), None))
+
+
+def from_cube(owner):
+    targets, relay = ROUTES[owner]
+
+    def spread(half):
+        held = jnp.where(lax.axis_index("zh") == owner, half, jnp.zeros_like(half))
+        for part in [lax.ppermute(half, "zh", [(owner, to)]) for to in targets]:
+            held = held + part
+        if relay:
+            held = held + lax.ppermute(held, "zh", [relay])
+        return held
+
+    return spread
+
+
+def from_all_cubes(half):
+    return lax.all_gather(half, "zh").sum(axis=0)
+
+
+def panel_of(half, offset, cols):
+    first = offset // (2 * cols)
+    last = (offset + PANEL - 1) // (2 * cols)
+    case = jnp.where(first == last, first, 4)
+    return lax.switch(case, [from_cube(zh) for zh in range(4)] + [from_all_cubes], half)
+
+
 def shards(environment, site_tensors, panel_offset):
     rows = environment.shape[0]
     cols = environment.shape[1]
@@ -49,7 +77,7 @@
     sent = jnp.concatenate([window(1 - core), environment], axis=1)
     came = swap(sent)
     half = window(core) + came[:, :PANEL]
-    panel = lax.all_gather(half, "zh").sum(axis=0)
+    panel = panel_of(half, panel_offset[0], cols)
 
     def bond(block):
         return jnp.einsum("ij,ip->jp", block, panel, precision=lax.Precision.HIGHEST)

time: 101 us -> 98.5 us (0.975); the launches traced: 100 us -> 100 us
  waiting for transfers between devices: 3.45 us -> 20.6 us
  blocking collectives: 69.6 us -> 56.6 us
  starting transfers between devices: 22 us -> 17.7 us
    all_gather x1 -> x0, blocking collectives: 18.1 us -> none  [shards(): panel = lax.all_gather(half, 'zh').sum(axis=0)]
    ppermute x0 -> x3, waiting for transfers between devices: none -> 13.8 us  [spread(): lax.ppermute(half, 'zh', [(owner, to)])]
    ppermute x2, starting transfers between devices: 16.6 us -> 13.2 us  [swap(): return lax.ppermute(values, 'core', [(0, 1), (1, 0)])]
    ppermute x1, starting transfers between devices: 5.37 us -> 1.92 us  [shards(): mine = lax.ppermute(piece, ALL, deliveries())]
    ppermute x1, waiting for transfers between devices: 1.86 us -> 5.31 us  [shards(): mine = lax.ppermute(piece, ALL, deliveries())]
    all_to_all x1, blocking collectives: 8.37 us -> 11.3 us  [shards(): piece = lax.all_to_all(copies, 'zl', 0, 0, tiled=True).sum(axis=0)]
    ppermute x0 -> x3, starting transfers between devices: none -> 2.62 us  [spread(): lax.ppermute(half, 'zh', [(owner, to)])]
    all_to_all x1, blocking collectives: 17 us -> 19.1 us  [shards(): pieces = lax.all_to_all(pieces, ('y', 'x'), 0, 0, tiled=True)]
  transfers between devices with their start and end apart: 3 -> 6, of which waited for: 3 -> 4; matrix products, arithmetic and copies ran while one was open for 1% -> 1% of each run, Pallas kernels for 0% -> 0%
where the time goes in v4:
time: 98.5 us; the launch traced here: 100 us
  blocking collectives  56.6 us (57%)
  waiting for transfers between devices  20.6 us (21%)
  starting transfers between devices  17.7 us (18%)
  matrix products  2.08 us (2%)
  local copies, waits for them, and re-layouts  1.44 us (1%)
  other arithmetic  1 us (1%)
    all_to_all x1, blocking collectives, shards(): shares = lax.all_to_all(total.reshape(64, 2, cols), ROW, 0, 0, tiled=True)  26.2 us
    all_to_all x1, blocking collectives, shards(): pieces = lax.all_to_all(pieces, ('y', 'x'), 0, 0, tiled=True)  19.1 us
    ppermute x3, waiting for transfers between devices, spread(): lax.ppermute(half, 'zh', [(owner, to)])  13.8 us
    ppermute x2, starting transfers between devices, swap(): return lax.ppermute(values, 'core', [(0, 1), (1, 0)])  13.2 us
    all_to_all x1, blocking collectives, shards(): piece = lax.all_to_all(copies, 'zl', 0, 0, tiled=True).sum(axis=0)  11.3 us
    ppermute x1, waiting for transfers between devices, shards(): mine = lax.ppermute(piece, ALL, deliveries())  5.31 us
    ppermute x3, starting transfers between devices, spread(): lax.ppermute(half, 'zh', [(owner, to)])  2.62 us
  transfers between devices with their start and end apart: 6, of which 4 were waited for; matrix products, arithmetic and copies ran while one was open for 1% of the time, Pallas kernels for 0%

profile of v4, /device:TPU:1, one launch (start us, length us, event | category | flops | bytes accessed | tf_op | source)
XLA Modules:
  0.0 100.4 jit_solution(9454654769820261798)
XLA Ops:
  0.7 0.0 copy-start.1
  0.7 0.0 copy-start
  0.7 0.1 fusion.7
  0.8 0.8 copy-done.1
  1.6 8.7 %collective-permute-start.12 = (f32[96,896]{1,0:T(8,128)S(1)}, f32[96,896]{1,0:T(8,128)S(1)}, u32[]{:S(2)}, u32[]{:S(2)}) collective-permute-start(f32[96,896]{1,0:T(8,128)S(1)} %pad_maximum_fusion.1), channel_id=1, source_target_pairs={{0,1},{1,0},{2,3},{3,2},{4,5},{5,4},{6,7},{7,6},{8,9},{9,8},{10,11... | collective-permute-start | bytes 1032200 | tf_op jit(solution)/shard_map/ppermute | solution.py:34
  10.4 1.2 %collective-permute-done.12 = f32[96,896]{1,0:T(8,128)S(1)} collective-permute-done((f32[96,896]{1,0:T(8,128)S(1)}, f32[96,896]{1,0:T(8,128)S(1)}, u32[]{:S(2)}, u32[]{:S(2)}) %collective-permute-start.12) | collective-permute-done | bytes 344096 | tf_op jit(solution)/shard_map/ppermute | solution.py:34
  11.7 0.0 copy-done
  11.7 0.1 slice_add_fusion
  11.7 16.5 %conditional.1 = (f32[96,128]{1,0:T(8,128)S(1)}) conditional(s32[]{:T(128)} %clamp.3, f32[96,128]{1,0:T(8,128)S(1)} %slice_add_fusion, f32[96,128]{1,0:T(8,128)S(1)} %slice_add_fusion, f32[96,128]{1,0:T(8,128)S(1)} %slice_add_fusion, f32[96,128]{1,0:T(8,128)S(1)} %slice_add_fusion, ...), branch_computations={%region_0.1_spmd, %region_1.2_spmd, %region_2.3_spmd, %region_3.4_... | conditional | flops 49156 | bytes 934058 | solution.py:62
  11.8 0.7 collective-permute-start.8
  12.4 0.7 collective-permute-start.7
  13.1 1.3 %collective-permute-start.6 = (f32[96,128]{1,0:T(8,128)S(1)}, f32[96,128]{1,0:T(8,128)S(1)}, u32[]{:S(2)}, u32[]{:S(2)}) collective-permute-start(f32[96,128]{1,0:T(8,128)S(1)} %param.2), channel_id=1, source_target_pairs={{4,0},{5,1},{12,8},{13,9},{20,16},{21,17},{28,24},{29,25},{36,32},... | collective-permute-start | bytes 147464 | tf_op jit(solution)/shard_map/cond/branch_2_fun/ppermute | solution.py:45
  14.4 0.0 collective-permute-done.8
  14.4 0.0 collective-permute-done.7
  14.4 13.8 %collective-permute-done.6 = f32[96,128]{1,0:T(8,128)S(1)} collective-permute-done((f32[96,128]{1,0:T(8,128)S(1)}, f32[96,128]{1,0:T(8,128)S(1)}, u32[]{:S(2)}, u32[]{:S(2)}) %collective-permute-start.6) | collective-permute-done | bytes 49184 | tf_op jit(solution)/shard_map/cond/branch_2_fun/ppermute | solution.py:45
  28.3 0.5 convolution_bitcast_fusion
  28.8 0.5 fusion
  29.3 0.1 pad_maximum_fusion
  29.4 0.3 copy.8
  29.7 19.1 %all_to_all.15 = f32[16,96,128]{2,1,0:T(8,128)S(1)} all-to-all(f32[16,96,128]{2,1,0:T(8,128)S(1)} %bitcast.25), channel_id=1, replica_groups=mesh['y'=4,'zl'=4,'x'=4,'zh'=4,'core'=2] {'y','x'}, dimensions={0} | all-to-all | bytes 1572864 | tf_op jit(solution)/shard_map/all_to_all | solution.py:87
  48.8 11.3 %all_to_all.16 = f32[4,96,128]{2,1,0:T(8,128)S(1)} all-to-all(f32[4,96,128]{2,1,0:T(8,128)S(1)} %broadcast_in_dim.2), channel_id=1, replica_groups=mesh['y'=4,'zl'=4,'x'=4,'zh'=4,'core'=2] {'zl'}, dimensions={0} | all-to-all | bytes 393216 | tf_op jit(solution)/shard_map/all_to_all | solution.py:90
  60.2 1.9 %collective-permute-start.13 = (f32[96,128]{1,0:T(8,128)S(1)}, f32[96,128]{1,0:T(8,128)S(1)}, u32[]{:S(2)}, u32[]{:S(2)}) collective-permute-start(f32[96,128]{1,0:T(8,128)S(1)} %reduce_sum.37), channel_id=1, source_target_pairs={{0,6},{1,69},{2,128},{3,199},{4,258},{5,321},{6,388},{7,451},{8,14... | collective-permute-start | bytes 147464 | tf_op jit(solution)/shard_map/ppermute | solution.py:91
  62.1 5.3 %collective-permute-done.13 = f32[96,128]{1,0:T(8,128)S(1)} collective-permute-done((f32[96,128]{1,0:T(8,128)S(1)}, f32[96,128]{1,0:T(8,128)S(1)}, u32[]{:S(2)}, u32[]{:S(2)}) %collective-permute-start.13) | collective-permute-done | bytes 49184 | tf_op jit(solution)/shard_map/ppermute | solution.py:91
  67.4 4.4 %collective-permute-start.14 = (f32[96,128]{1,0:T(8,128)S(1)}, f32[96,128]{1,0:T(8,128)S(1)}, u32[]{:S(2)}, u32[]{:S(2)}) collective-permute-start(f32[96,128]{1,0:T(8,128)S(1)} %collective-permute-done.13), channel_id=1, source_target_pairs={{0,1},{1,0},{2,3},{3,2},{4,5},{5,4},{6,7},{7,6},{8,9},{9,8},{10,11... | collective-permute-start | bytes 147464 | tf_op jit(solution)/shard_map/ppermute | solution.py:34
  71.8 0.5 fusion.3
  72.4 0.3 collective-permute-done.14
  72.7 0.5 convolution_add_fusion
  73.2 0.2 reshape.8
  73.5 26.2 %all_to_all.17 = f32[64,2,768]{2,1,0:T(2,128)S(1)} all-to-all(f32[64,2,768]{2,1,0:T(2,128)S(1)} %reshape.8), channel_id=1, replica_groups=mesh['y'=4,'zl'=4,'x'=4,'zh'=4,'core'=2] {'y','zl','x'}, dimensions={0} | all-to-all | bytes 786432 | tf_op jit(solution)/shard_map/all_to_all | solution.py:99
  99.6 0.7 reduce_sum.38
  (5 shorter events, 0.1 us)
Async XLA Ops:
  0.7 1.0 copy-start.1
  0.7 11.0 %copy-start = (f32[2,96,768]{2,1,0:T(8,128)S(1)}, f32[2,96,768]{2,1,0:T(8,128)}, u32[]{:S(2)}) copy-start(f32[2,96,768]{2,1,0:T(8,128)} %param.9) | copy-start | bytes 1769476
  1.6 10.0 %collective-permute-start.12 = (f32[96,896]{1,0:T(8,128)S(1)}, f32[96,896]{1,0:T(8,128)S(1)}, u32[]{:S(2)}, u32[]{:S(2)}) collective-permute-start(f32[96,896]{1,0:T(8,128)S(1)} %pad_maximum_fusion.1), channel_id=1, source_target_pairs={{0,1},{1,0},{2,3},{3,2},{4,5},{5,4},{6,7},{7,6},{8,9},{9,8},{10,11... | collective-permute-start | bytes 1032200 | tf_op jit(solution)/shard_map/ppermute | solution.py:34
  11.8 2.7 %collective-permute-start.8 = (f32[96,128]{1,0:T(8,128)S(1)}, f32[96,128]{1,0:T(8,128)S(1)}, u32[]{:S(2)}, u32[]{:S(2)}) collective-permute-start(f32[96,128]{1,0:T(8,128)S(1)} %param.2), channel_id=1, source_target_pairs={{4,6},{5,7},{12,14},{13,15},{20,22},{21,23},{28,30},{29,31},{36,38... | collective-permute-start | bytes 147464 | tf_op jit(solution)/shard_map/cond/branch_2_fun/ppermute | solution.py:45
  12.4 2.0 %collective-permute-start.7 = (f32[96,128]{1,0:T(8,128)S(1)}, f32[96,128]{1,0:T(8,128)S(1)}, u32[]{:S(2)}, u32[]{:S(2)}) collective-permute-start(f32[96,128]{1,0:T(8,128)S(1)} %param.2), channel_id=1, source_target_pairs={{4,2},{5,3},{12,10},{13,11},{20,18},{21,19},{28,26},{29,27},{36,34... | collective-permute-start | bytes 147464 | tf_op jit(solution)/shard_map/cond/branch_2_fun/ppermute | solution.py:45
  13.1 15.1 %collective-permute-start.6 = (f32[96,128]{1,0:T(8,128)S(1)}, f32[96,128]{1,0:T(8,128)S(1)}, u32[]{:S(2)}, u32[]{:S(2)}) collective-permute-start(f32[96,128]{1,0:T(8,128)S(1)} %param.2), channel_id=1, source_target_pairs={{4,0},{5,1},{12,8},{13,9},{20,16},{21,17},{28,24},{29,25},{36,32},... | collective-permute-start | bytes 147464 | tf_op jit(solution)/shard_map/cond/branch_2_fun/ppermute | solution.py:45
  60.2 7.2 %collective-permute-start.13 = (f32[96,128]{1,0:T(8,128)S(1)}, f32[96,128]{1,0:T(8,128)S(1)}, u32[]{:S(2)}, u32[]{:S(2)}) collective-permute-start(f32[96,128]{1,0:T(8,128)S(1)} %reduce_sum.37), channel_id=1, source_target_pairs={{0,6},{1,69},{2,128},{3,199},{4,258},{5,321},{6,388},{7,451},{8,14... | collective-permute-start | bytes 147464 | tf_op jit(solution)/shard_map/ppermute | solution.py:91
  67.4 5.3 %collective-permute-start.14 = (f32[96,128]{1,0:T(8,128)S(1)}, f32[96,128]{1,0:T(8,128)S(1)}, u32[]{:S(2)}, u32[]{:S(2)}) collective-permute-start(f32[96,128]{1,0:T(8,128)S(1)} %collective-permute-done.13), channel_id=1, source_target_pairs={{0,1},{1,0},{2,3},{3,2},{4,5},{5,4},{6,7},{7,6},{8,9},{9,8},{10,11... | collective-permute-start | bytes 147464 | tf_op jit(solution)/shard_map/ppermute | solution.py:34

commit v5 on v4

--- a/solution.py
+++ b/solution.py
@@ -1,6 +1,8 @@
 import jax
 import jax.numpy as jnp
 from jax import lax
+from jax.experimental import pallas as pl
+from jax.experimental.pallas import tpu as pltpu
 from jax.sharding import Mesh, PartitionSpec as P
 
 PHYS = 2
@@ -16,18 +18,88 @@
     return (((y * 4 + zl) * 4 + x) * 4 + zh) * 2 + core
 
 
+SHIFT = (2, 0, 3, 1)
+TARGET = (1, 3, 0, 2)
+
+
 def deliveries():
     pairs = []
     for y in range(4):
-        far, b = y // 2, y % 2
         for zl in range(4):
             for x in range(4):
                 for zh in range(4):
+                    to = TARGET[(y - zh) % 4]
                     for core in range(2):
-                        to = 2 * (core ^ far) + b
                         there = flat(zh, to, x, (zh + HOPS[to][zl]) % 4, core)
                         pairs.append((flat(y, zl, x, zh, core), there))
     return pairs
+
+
+SMALL = pltpu.CompilerParams(vmem_limit_bytes=8 * 2**20)
+
+
+def halves(values):
+    high = values.astype(jnp.bfloat16)
+    return high, (values - high.astype(jnp.float32)).astype(jnp.bfloat16)
+
+
+def product(left, right):
+    dot = lambda a, b: jnp.dot(a, b, preferred_element_type=jnp.float32)
+    (lh, ll), (rh, rl) = halves(left), halves(right)
+    return dot(lh, rh) + (dot(lh, rl) + dot(ll, rh))
+
+
+def bond_kernel(panel_ref, sent_ref, came_ref, out_ref):
+    core, zh = lax.axis_index("core"), lax.axis_index("zh")
+    panel = panel_ref[...].T
+    count = out_ref.shape[1]
+    for far, ref in ((0, sent_ref), (1, came_ref)):
+        block = product(panel, ref[:, PANEL:])
+        for b in range(2):
+            to = 2 * (core ^ far) + b
+            shift = jnp.where(to == 0, 2, jnp.where(to == 1, 0, jnp.where(to == 2, 3, 1)))
+            y = (zh + shift) % 4
+            for x in range(4):
+                start = (4 * b + x) * count
+                out_ref[4 * y + x] = block[:, start : start + count].T
+
+
+def bond(panel, sent, came):
+    rows = panel.shape[0]
+    return pl.pallas_call(
+        bond_kernel,
+        out_shape=jax.ShapeDtypeStruct((16, rows, PANEL), jnp.float32),
+        in_specs=[pl.BlockSpec(memory_space=pltpu.VMEM)] * 3,
+        out_specs=pl.BlockSpec(memory_space=pltpu.VMEM),
+        compiler_params=SMALL,
+        name="bond",
+    )(panel, sent, came)
+
+
+def mine_kernel(block_ref, tensors_ref, out_ref):
+    core = lax.axis_index("core")
+    out_ref[...] = product(block_ref[...].T, tensors_ref[core])
+
+
+def other_kernel(block_ref, tensors_ref, sum_ref, out_ref):
+    core = lax.axis_index("core")
+    total = sum_ref[...] + product(block_ref[...].T, tensors_ref[1 - core])
+    out_ref[...] = total.reshape(out_ref.shape)
+
+
+def times(kernel, shape, *operands):
+    return pl.pallas_call(
+        kernel,
+        out_shape=jax.ShapeDtypeStruct(shape, jnp.float32),
+        in_specs=[pl.BlockSpec(memory_space=pltpu.VMEM)] * len(operands),
+        out_specs=pl.BlockSpec(memory_space=pltpu.VMEM),
+        compiler_params=SMALL,
+        name=kernel.__name__,
+    )(*operands)
+
+
+def add_kernel(shares_ref, out_ref):
+    out_ref[...] = jnp.sum(shares_ref[...], axis=0)
 
 
 def swap(values):
@@ -79,11 +151,7 @@
     half = window(core) + came[:, :PANEL]
     panel = panel_of(half, panel_offset[0], cols)
 
-    def bond(block):
-        return jnp.einsum("ij,ip->jp", block, panel, precision=lax.Precision.HIGHEST)
-
-    pieces = jnp.concatenate([bond(environment), bond(came[:, PANEL:])], axis=0)
-    pieces = pieces.reshape(16, rows, PANEL)
+    pieces = bond(panel, sent, came)
     pieces = lax.all_to_all(pieces, ("y", "x"), 0, 0, tiled=True)
     piece = pieces.sum(axis=0)
     copies = jnp.broadcast_to(piece[None], (4, rows, PANEL))
@@ -91,13 +159,10 @@
     mine = lax.ppermute(piece, ALL, deliveries())
     other = swap(mine)
 
-    def times(block, phys):
-        tensor = lax.dynamic_index_in_dim(site_tensors, phys, 0, keepdims=False)
-        return jnp.einsum("jp,jm->pm", block, tensor, precision=lax.Precision.HIGHEST)
-
-    total = times(mine, core) + times(other, 1 - core)
-    shares = lax.all_to_all(total.reshape(64, 2, cols), ROW, 0, 0, tiled=True)
-    return shares.sum(axis=0)
+    total = times(mine_kernel, (PANEL, cols), mine, site_tensors)
+    total = times(other_kernel, (64, 2, cols), other, site_tensors, total)
+    shares = lax.all_to_all(total, ROW, 0, 0, tiled=True)
+    return times(add_kernel, (2, cols), shares)
 
 
 def solution(mesh):

time: 98.5 us -> 96.7 us (0.982); the launches traced: 100 us -> 95.3 us
  starting transfers between devices: 17.7 us -> 27.5 us
  blocking collectives: 56.6 us -> 49.1 us
  waiting for transfers between devices: 20.6 us -> 14.1 us
  Pallas kernels: 0 us -> 2.61 us
  matrix products: 2.08 us -> 0 us
    ppermute x1, starting transfers between devices: 1.92 us -> 7.22 us  [shards(): mine = lax.ppermute(piece, ALL, deliveries())]
    all_to_all x1, blocking collectives: 26.2 us -> 21.3 us  [shards(): shares = lax.all_to_all(total, ROW, 0, 0, tiled=True)]
    ppermute x2, starting transfers between devices: 13.2 us -> 17.7 us  [swap(): return lax.ppermute(values, 'core', [(0, 1), (1, 0)])]
    ppermute x1, waiting for transfers between devices: 5.31 us -> 1.16 us  [shards(): mine = lax.ppermute(piece, ALL, deliveries())]
    pallas_call x0 -> x4, Pallas kernels: none -> 2.61 us  [the longest x3 1.51 us: times(): pl.pallas_call(kernel, out_shape=jax.ShapeDtypeStruct(shape, jnp.float32)...]
    ppermute x3 -> x2, waiting for transfers between devices: 13.8 us -> 11.2 us  [spread(): lax.ppermute(half, 'zh', [(owner, to)])]
    all_to_all x1, blocking collectives: 19.1 us -> 17 us  [shards(): pieces = lax.all_to_all(pieces, ('y', 'x'), 0, 0, tiled=True)]
    dot_general x4 -> x0, matrix products: 2.08 us -> none  [the longest x2 1.05 us: times(): jnp.einsum('jp,jm->pm', block, tensor, precision=lax.Precision.HIGHEST)]
  transfers between devices with their start and end apart: 6 -> 6, of which waited for: 4 -> 4; matrix products, arithmetic and copies ran while one was open for 1% -> 0% of each run, Pallas kernels for 0% -> 0%
where the time goes in v5:
time: 96.7 us; the launch traced here: 95.3 us
  blocking collectives  49.1 us (51%)
  starting transfers between devices  27.5 us (28%)
  waiting for transfers between devices  14.1 us (15%)
  Pallas kernels  2.61 us (3%)
    all_to_all x1, blocking collectives, shards(): shares = lax.all_to_all(total, ROW, 0, 0, tiled=True)  21.3 us
    ppermute x2, starting transfers between devices, swap(): return lax.ppermute(values, 'core', [(0, 1), (1, 0)])  17.7 us
    all_to_all x1, blocking collectives, shards(): pieces = lax.all_to_all(pieces, ('y', 'x'), 0, 0, tiled=True)  17 us
    ppermute x2, waiting for transfers between devices, spread(): lax.ppermute(half, 'zh', [(owner, to)])  11.2 us
    all_to_all x1, blocking collectives, shards(): piece = lax.all_to_all(copies, 'zl', 0, 0, tiled=True).sum(axis=0)  10.7 us
    ppermute x1, starting transfers between devices, shards(): mine = lax.ppermute(piece, ALL, deliveries())  7.22 us
    ppermute x2, starting transfers between devices, spread(): lax.ppermute(half, 'zh', [(owner, to)])  1.96 us
  transfers between devices with their start and end apart: 6, of which 4 were waited for; matrix products, arithmetic and copies ran while one was open for 0% of the time, Pallas kernels for 0%

profile of v5, /device:TPU:1, one launch (start us, length us, event | category | flops | bytes accessed | tf_op | source)
XLA Modules:
  0.0 95.3 jit_solution(16872596667994088177)
XLA Ops:
  0.7 0.0 copy-start.1
  0.7 0.0 copy-start
  0.7 0.1 fusion
  0.8 0.8 copy-done.1
  1.6 8.7 %collective-permute-start.12 = (f32[96,896]{1,0:T(8,128)S(1)}, f32[96,896]{1,0:T(8,128)S(1)}, u32[]{:S(2)}, u32[]{:S(2)}) collective-permute-start(f32[96,896]{1,0:T(8,128)S(1)} %pad_maximum_fusion.sent_ref), channel_id=1, source_target_pairs={{0,1},{1,0},{2,3},{3,2},{4,5},{5,4},{6,7},{7,6},{8,9},{9,8},{10,11... | collective-permute-start | bytes 1032200 | tf_op jit(solution)/shard_map/ppermute | solution.py:106
  10.4 1.2 %collective-permute-done.12.came_ref = f32[96,896]{1,0:T(8,128)S(1)} collective-permute-done((f32[96,896]{1,0:T(8,128)S(1)}, f32[96,896]{1,0:T(8,128)S(1)}, u32[]{:S(2)}, u32[]{:S(2)}) %collective-permute-start.12) | collective-permute-done | bytes 344096 | tf_op jit(solution)/shard_map/ppermute | solution.py:106
  11.7 0.0 copy-done
  11.7 0.1 slice_add_fusion
  11.7 13.9 %conditional.1 = (f32[96,128]{1,0:T(8,128)S(1)}) conditional(s32[]{:T(128)} %clamp.3, f32[96,128]{1,0:T(8,128)S(1)} %slice_add_fusion, f32[96,128]{1,0:T(8,128)S(1)} %slice_add_fusion, f32[96,128]{1,0:T(8,128)S(1)} %slice_add_fusion, f32[96,128]{1,0:T(8,128)S(1)} %slice_add_fusion, ...), branch_computations={%region_0.1_spmd, %region_1.2_spmd, %region_2.3_spmd, %region_3.4_... | conditional | flops 49156 | bytes 934058 | solution.py:134
  11.8 0.7 collective-permute-start.4
  12.4 1.3 %collective-permute-start.3 = (f32[96,128]{1,0:T(8,128)S(1)}, f32[96,128]{1,0:T(8,128)S(1)}, u32[]{:S(2)}, u32[]{:S(2)}) collective-permute-start(f32[96,128]{1,0:T(8,128)S(1)} %param.1), channel_id=1, source_target_pairs={{2,0},{3,1},{10,8},{11,9},{18,16},{19,17},{26,24},{27,25},{34,32},... | collective-permute-start | bytes 147464 | tf_op jit(solution)/shard_map/cond/branch_1_fun/ppermute | solution.py:117
  13.8 0.0 collective-permute-done.4
  13.8 11.2 %collective-permute-done.3 = f32[96,128]{1,0:T(8,128)S(1)} collective-permute-done((f32[96,128]{1,0:T(8,128)S(1)}, f32[96,128]{1,0:T(8,128)S(1)}, u32[]{:S(2)}, u32[]{:S(2)}) %collective-permute-start.3) | collective-permute-done | bytes 49184 | tf_op jit(solution)/shard_map/cond/branch_1_fun/ppermute | solution.py:117
  25.0 0.7 collective-permute-start.5
  25.7 0.0 collective-permute-done.5
  25.7 1.1 %bond.1 = f32[16,96,128]{2,1,0:T(8,128)S(1)} custom-call(f32[96,128]{1,0:T(8,128)S(1)} %get-tuple-element.16.panel_ref, f32[96,896]{1,0:T(8,128)S(1)} %pad_maximum_fusion.sent_ref, f32[96,896]{1,0:T(8,128)S(1)} %collective-permute-done.12.came_ref), custom_call_target="tpu_custom_call" | custom-call | tf_op jit(solution)/shard_map/bond/pallas_call | solution.py:69
  26.8 17.0 %all_to_all.15 = f32[16,96,128]{2,1,0:T(8,128)S(1)} all-to-all(f32[16,96,128]{2,1,0:T(8,128)S(1)} %bond.1), channel_id=1, replica_groups=mesh['y'=4,'zl'=4,'x'=4,'zh'=4,'core'=2] {'y','x'}, dimensions={0} | all-to-all | bytes 1572864 | tf_op jit(solution)/shard_map/all_to_all | solution.py:155
  43.9 10.7 %all_to_all.16 = f32[4,96,128]{2,1,0:T(8,128)S(1)} all-to-all(f32[4,96,128]{2,1,0:T(8,128)S(1)} %broadcast_in_dim.2), channel_id=1, replica_groups=mesh['y'=4,'zl'=4,'x'=4,'zh'=4,'core'=2] {'zl'}, dimensions={0} | all-to-all | bytes 393216 | tf_op jit(solution)/shard_map/all_to_all | solution.py:158
  54.6 7.2 %collective-permute-start.13 = (f32[96,128]{1,0:T(8,128)S(1)}, f32[96,128]{1,0:T(8,128)S(1)}, u32[]{:S(2)}, u32[]{:S(2)}) collective-permute-start(f32[96,128]{1,0:T(8,128)S(1)} %reduce_sum.28), channel_id=1, source_target_pairs={{0,38},{1,39},{2,198},{3,199},{4,258},{5,259},{6,482},{7,483},{8,4... | collective-permute-start | bytes 147464 | tf_op jit(solution)/shard_map/ppermute | solution.py:159
  61.8 1.2 %collective-permute-done.13.block_ref = f32[96,128]{1,0:T(8,128)S(1)} collective-permute-done((f32[96,128]{1,0:T(8,128)S(1)}, f32[96,128]{1,0:T(8,128)S(1)}, u32[]{:S(2)}, u32[]{:S(2)}) %collective-permute-start.13) | collective-permute-done | bytes 49184 | tf_op jit(solution)/shard_map/ppermute | solution.py:159
  63.0 8.9 %collective-permute-start.14 = (f32[96,128]{1,0:T(8,128)S(1)}, f32[96,128]{1,0:T(8,128)S(1)}, u32[]{:S(2)}, u32[]{:S(2)}) collective-permute-start(f32[96,128]{1,0:T(8,128)S(1)} %collective-permute-done.13.block_ref), channel_id=1, source_target_pairs={{0,1},{1,0},{2,3},{3,2},{4,5},{5,4},{6,7},{7,6},{8,9},{9,8},{10,11... | collective-permute-start | bytes 147464 | tf_op jit(solution)/shard_map/ppermute | solution.py:106
  71.9 0.4 mine_kernel.1.sum_ref
  72.3 0.5 collective-permute-done.14.block_ref
  72.8 0.4 other_kernel.1
  73.2 21.3 %all_to_all.17.shares_ref = f32[64,2,768]{2,1,0:T(2,128)S(1)} all-to-all(f32[64,2,768]{2,1,0:T(2,128)S(1)} %other_kernel.1), channel_id=1, replica_groups=mesh['y'=4,'zl'=4,'x'=4,'zh'=4,'core'=2] {'y','zl','x'}, dimensions={0} | all-to-all | bytes 786432 | tf_op jit(solution)/shard_map/all_to_all | solution.py:164
  94.5 0.8 add_kernel.1
  (6 shorter events, 0.1 us)
Async XLA Ops:
  0.7 1.0 %copy-start.1 = (f32[96,768]{1,0:T(8,128)S(1)}, f32[96,768]{1,0:T(8,128)}, u32[]{:S(2)}) copy-start(f32[96,768]{1,0:T(8,128)} %param.8) | copy-start | bytes 884740
  0.7 11.0 %copy-start = (f32[2,96,768]{2,1,0:T(8,128)S(1)}, f32[2,96,768]{2,1,0:T(8,128)}, u32[]{:S(2)}) copy-start(f32[2,96,768]{2,1,0:T(8,128)} %tensors_ref.3) | copy-start | bytes 1769476
  1.6 10.0 %collective-permute-start.12 = (f32[96,896]{1,0:T(8,128)S(1)}, f32[96,896]{1,0:T(8,128)S(1)}, u32[]{:S(2)}, u32[]{:S(2)}) collective-permute-start(f32[96,896]{1,0:T(8,128)S(1)} %pad_maximum_fusion.sent_ref), channel_id=1, source_target_pairs={{0,1},{1,0},{2,3},{3,2},{4,5},{5,4},{6,7},{7,6},{8,9},{9,8},{10,11... | collective-permute-start | bytes 1032200 | tf_op jit(solution)/shard_map/ppermute | solution.py:106
  11.8 2.0 %collective-permute-start.4 = (f32[96,128]{1,0:T(8,128)S(1)}, f32[96,128]{1,0:T(8,128)S(1)}, u32[]{:S(2)}, u32[]{:S(2)}) collective-permute-start(f32[96,128]{1,0:T(8,128)S(1)} %param.1), channel_id=1, source_target_pairs={{2,4},{3,5},{10,12},{11,13},{18,20},{19,21},{26,28},{27,29},{34,36... | collective-permute-start | bytes 147464 | tf_op jit(solution)/shard_map/cond/branch_1_fun/ppermute | solution.py:117
  12.4 12.5 %collective-permute-start.3 = (f32[96,128]{1,0:T(8,128)S(1)}, f32[96,128]{1,0:T(8,128)S(1)}, u32[]{:S(2)}, u32[]{:S(2)}) collective-permute-start(f32[96,128]{1,0:T(8,128)S(1)} %param.1), channel_id=1, source_target_pairs={{2,0},{3,1},{10,8},{11,9},{18,16},{19,17},{26,24},{27,25},{34,32},... | collective-permute-start | bytes 147464 | tf_op jit(solution)/shard_map/cond/branch_1_fun/ppermute | solution.py:117
  25.0 0.7 collective-permute-start.5
  54.6 8.4 %collective-permute-start.13 = (f32[96,128]{1,0:T(8,128)S(1)}, f32[96,128]{1,0:T(8,128)S(1)}, u32[]{:S(2)}, u32[]{:S(2)}) collective-permute-start(f32[96,128]{1,0:T(8,128)S(1)} %reduce_sum.28), channel_id=1, source_target_pairs={{0,38},{1,39},{2,198},{3,199},{4,258},{5,259},{6,482},{7,483},{8,4... | collective-permute-start | bytes 147464 | tf_op jit(solution)/shard_map/ppermute | solution.py:159
  63.0 9.8 %collective-permute-start.14 = (f32[96,128]{1,0:T(8,128)S(1)}, f32[96,128]{1,0:T(8,128)S(1)}, u32[]{:S(2)}, u32[]{:S(2)}) collective-permute-start(f32[96,128]{1,0:T(8,128)S(1)} %collective-permute-done.13.block_ref), channel_id=1, source_target_pairs={{0,1},{1,0},{2,3},{3,2},{4,5},{5,4},{6,7},{7,6},{8,9},{9,8},{10,11... | collective-permute-start | bytes 147464 | tf_op jit(solution)/shard_map/ppermute | solution.py:106

commit v6 on v5

--- a/solution.py
+++ b/solution.py
@@ -5,7 +5,7 @@
 from jax.experimental.pallas import tpu as pltpu
 from jax.sharding import Mesh, PartitionSpec as P
 
-PHYS = 2
+
 PANEL = 128
 ROW = ("y", "zl", "x")
 COL = ("zh", "core")
@@ -18,7 +18,6 @@
     return (((y * 4 + zl) * 4 + x) * 4 + zh) * 2 + core
 
 
-SHIFT = (2, 0, 3, 1)
 TARGET = (1, 3, 0, 2)
 
 
@@ -49,12 +48,12 @@
     return dot(lh, rh) + (dot(lh, rl) + dot(ll, rh))
 
 
-def bond_kernel(panel_ref, sent_ref, came_ref, out_ref):
+def bond_kernel(panel_ref, own_ref, came_ref, out_ref):
     core, zh = lax.axis_index("core"), lax.axis_index("zh")
     panel = panel_ref[...].T
     count = out_ref.shape[1]
-    for far, ref in ((0, sent_ref), (1, came_ref)):
-        block = product(panel, ref[:, PANEL:])
+    for far, ref in ((0, own_ref), (1, came_ref)):
+        block = product(panel, ref[...])
         for b in range(2):
             to = 2 * (core ^ far) + b
             shift = jnp.where(to == 0, 2, jnp.where(to == 1, 0, jnp.where(to == 2, 3, 1)))
@@ -64,7 +63,7 @@
                 out_ref[4 * y + x] = block[:, start : start + count].T
 
 
-def bond(panel, sent, came):
+def bond(panel, own, came):
     rows = panel.shape[0]
     return pl.pallas_call(
         bond_kernel,
@@ -73,7 +72,7 @@
         out_specs=pl.BlockSpec(memory_space=pltpu.VMEM),
         compiler_params=SMALL,
         name="bond",
-    )(panel, sent, came)
+    )(panel, own, came)
 
 
 def mine_kernel(block_ref, tensors_ref, out_ref):
@@ -94,7 +93,6 @@
         in_specs=[pl.BlockSpec(memory_space=pltpu.VMEM)] * len(operands),
         out_specs=pl.BlockSpec(memory_space=pltpu.VMEM),
         compiler_params=SMALL,
-        name=kernel.__name__,
     )(*operands)
 
 
@@ -102,36 +100,39 @@
     out_ref[...] = jnp.sum(shares_ref[...], axis=0)
 
 
+TARGETS = ((1, 3, 2), (0, 2, 3), (0, 1, 3), (0, 1, 2))
+
+
 def swap(values):
     return lax.ppermute(values, "core", [(0, 1), (1, 0)])
 
 
-ROUTES = (((2, 1, 3), None), ((0, 2), (2, 3)), ((0, 1, 3), None), ((1, 0, 2), None))
-
-
 def from_cube(owner):
-    targets, relay = ROUTES[owner]
-
-    def spread(half):
+    def spread(kept, sent, environment):
+        pair = [(2 * owner, 2 * owner + 1), (2 * owner + 1, 2 * owner)]
+        half = kept + lax.ppermute(sent, COL, pair)
         held = jnp.where(lax.axis_index("zh") == owner, half, jnp.zeros_like(half))
-        for part in [lax.ppermute(half, "zh", [(owner, to)]) for to in targets]:
+        parts = [lax.ppermute(half, "zh", [(owner, to)]) for to in TARGETS[owner]]
+        came = lax.ppermute(environment, "core", [(0, 1), (1, 0)])
+        for part in parts:
             held = held + part
-        if relay:
-            held = held + lax.ppermute(held, "zh", [relay])
-        return held
+        return held, came
 
     return spread
 
 
-def from_all_cubes(half):
-    return lax.all_gather(half, "zh").sum(axis=0)
+def from_all_cubes(kept, sent, environment):
+    half = kept + swap(sent)
+    return lax.all_gather(half, "zh").sum(axis=0), swap(environment)
 
 
-def panel_of(half, offset, cols):
-    first = offset // (2 * cols)
-    last = (offset + PANEL - 1) // (2 * cols)
+def panel_of(kept, sent, environment, offset):
+    cols = 2 * environment.shape[1]
+    first = offset // cols
+    last = (offset + PANEL - 1) // cols
     case = jnp.where(first == last, first, 4)
-    return lax.switch(case, [from_cube(zh) for zh in range(4)] + [from_all_cubes], half)
+    branches = [from_cube(zh) for zh in range(4)] + [from_all_cubes]
+    return lax.switch(case, branches, kept, sent, environment)
 
 
 def shards(environment, site_tensors, panel_offset):
@@ -146,12 +147,8 @@
     def window(phys):
         return lax.dynamic_slice(padded, (phys, zero, start), (1, rows, PANEL))[0]
 
-    sent = jnp.concatenate([window(1 - core), environment], axis=1)
-    came = swap(sent)
-    half = window(core) + came[:, :PANEL]
-    panel = panel_of(half, panel_offset[0], cols)
-
-    pieces = bond(panel, sent, came)
+    panel, came = panel_of(window(core), window(1 - core), environment, panel_offset[0])
+    pieces = bond(panel, environment, came)
     pieces = lax.all_to_all(pieces, ("y", "x"), 0, 0, tiled=True)
     piece = pieces.sum(axis=0)
     copies = jnp.broadcast_to(piece[None], (4, rows, PANEL))

time: 96.7 us -> 102 us (1.055)
  waiting for transfers between devices: 14.1 us -> 23 us
  starting transfers between devices: 27.5 us -> 20.5 us
  blocking collectives: 49.1 us -> 52.1 us
    ppermute x2 -> x1, starting transfers between devices: 17.7 us -> 6.59 us  [swap(): return lax.ppermute(values, 'core', [(0, 1), (1, 0)])]
    ppermute x3 -> x5, starting transfers between devices: 2.62 us -> 12 us  [the longest x1 8.75 us: spread(): came = lax.ppermute(environment, 'core', [(0, 1), (1, 0)])]
    ppermute x3 -> x5, waiting for transfers between devices: 11.2 us -> 17.2 us  [the longest x3 17.2 us: spread(): parts = [lax.ppermute(half, 'zh', [(owner, to)]) for to in TARGETS[owner]]]
    ppermute x1, starting transfers between devices: 7.22 us -> 1.92 us  [shards(): mine = lax.ppermute(piece, ALL, deliveries())]
    ppermute x1, waiting for transfers between devices: 1.16 us -> 5.31 us  [shards(): mine = lax.ppermute(piece, ALL, deliveries())]
    all_to_all x1, blocking collectives: 17 us -> 20 us  [shards(): pieces = lax.all_to_all(pieces, ('y', 'x'), 0, 0, tiled=True)]
    all_to_all x1, blocking collectives: 21.3 us -> 24 us  [shards(): shares = lax.all_to_all(total, ROW, 0, 0, tiled=True)]
    all_to_all x1, blocking collectives: 10.7 us -> 8.15 us  [shards(): piece = lax.all_to_all(copies, 'zl', 0, 0, tiled=True).sum(axis=0)]
  transfers between devices with their start and end apart: 6 -> 7, of which waited for: 4 -> 3; matrix products, arithmetic and copies ran while one was open for 0% -> 0% of each run, Pallas kernels for 0% -> 0%
where the time goes in v6:
time: 102 us; the launch traced here: 101 us
  blocking collectives  52.1 us (51%)
  waiting for transfers between devices  23 us (23%)
  starting transfers between devices  20.5 us (20%)
  Pallas kernels  3.58 us (4%)
    all_to_all x1, blocking collectives, shards(): shares = lax.all_to_all(total, ROW, 0, 0, tiled=True)  24 us
    all_to_all x1, blocking collectives, shards(): pieces = lax.all_to_all(pieces, ('y', 'x'), 0, 0, tiled=True)  20 us
    ppermute x3, waiting for transfers between devices, spread(): parts = [lax.ppermute(half, 'zh', [(owner, to)]) for to in TARGETS[owner]]  17.2 us
    ppermute x1, starting transfers between devices, spread(): came = lax.ppermute(environment, 'core', [(0, 1), (1, 0)])  8.75 us
    all_to_all x1, blocking collectives, shards(): piece = lax.all_to_all(copies, 'zl', 0, 0, tiled=True).sum(axis=0)  8.15 us
    ppermute x1, starting transfers between devices, swap(): return lax.ppermute(values, 'core', [(0, 1), (1, 0)])  6.59 us
    ppermute x1, waiting for transfers between devices, shards(): mine = lax.ppermute(piece, ALL, deliveries())  5.31 us
    ppermute x3, starting transfers between devices, spread(): parts = [lax.ppermute(half, 'zh', [(owner, to)]) for to in TARGETS[owner]]  2.62 us
  transfers between devices with their start and end apart: 7, of which 3 were waited for; matrix products, arithmetic and copies ran while one was open for 0% of the time, Pallas kernels for 0%

profile of v6, /device:TPU:1, one launch (start us, length us, event | category | flops | bytes accessed | tf_op | source)
XLA Modules:
  0.0 101.1 jit_solution(11209242680675034750)
XLA Ops:
  0.7 0.0 copy-start.1
  0.7 0.1 fusion.1
  0.8 0.8 copy-done.1
  1.7 29.3 %conditional.1 = (f32[96,128]{1,0:T(8,128)S(1)}, f32[96,768]{1,0:T(8,128)}) conditional(s32[]{:T(128)} %clamp.3, (f32[96,128]{1,0:T(8,128)S(1)}, f32[96,128]{1,0:T(8,128)S(1)}, f32[96,768]{1,0:T(8,128)S(1)}) %tuple.32, (f32[96,128]{1,0:T(8,128)S(1)}, f32[96,128]{1,0:T(8,128)S(1)}, f32[96,768]{1,0:T(8,128)S(1)}) %tuple.33, ...), branch_computations={%region_0.1_spmd, %region_1.2_spmd, %region_2.3_spmd, %region_3.4_... | conditional | flops 61444 | bytes 2359554 | solution.py:135
  1.7 0.7 collective-permute-start.7
  2.3 8.7 %collective-permute-start.11 = (f32[96,768]{1,0:T(8,128)S(1)}, f32[96,768]{1,0:T(8,128)}, u32[]{:S(2)}, u32[]{:S(2)}) collective-permute-start(f32[96,768]{1,0:T(8,128)S(1)} %get-tuple-element.40), channel_id=1, source_target_pairs={{0,1},{1,0},{2,3},{3,2},{4,5},{5,4},{6,7},{7,6},{8,9},{9,8},{10,11... | collective-permute-start | bytes 884744 | tf_op jit(solution)/shard_map/cond/branch_1_fun/ppermute | solution.py:116
  11.1 0.0 collective-permute-done.7
  11.1 0.7 collective-permute-start.10
  11.8 0.7 collective-permute-start.9
  12.5 1.3 %collective-permute-start.8 = (f32[96,128]{1,0:T(8,128)S(1)}, f32[96,128]{1,0:T(8,128)S(1)}, u32[]{:S(2)}, u32[]{:S(2)}) collective-permute-start(f32[96,128]{1,0:T(8,128)S(1)} %add.55), channel_id=1, source_target_pairs={{2,0},{3,1},{10,8},{11,9},{18,16},{19,17},{26,24},{27,25},{34,32},... | collective-permute-start | bytes 147464 | tf_op jit(solution)/shard_map/cond/branch_1_fun/ppermute | solution.py:115
  13.8 0.0 collective-permute-done.10
  13.8 0.0 collective-permute-done.9
  13.8 17.2 %collective-permute-done.8 = f32[96,128]{1,0:T(8,128)S(1)} collective-permute-done((f32[96,128]{1,0:T(8,128)S(1)}, f32[96,128]{1,0:T(8,128)S(1)}, u32[]{:S(2)}, u32[]{:S(2)}) %collective-permute-start.8) | collective-permute-done | bytes 49184 | tf_op jit(solution)/shard_map/cond/branch_1_fun/ppermute | solution.py:115
  31.0 0.0 collective-permute-done.11
  31.0 2.1 %bond.1 = f32[16,96,128]{2,1,0:T(8,128)S(1)} custom-call(f32[96,128]{1,0:T(8,128)S(1)} %get-tuple-element.52.panel_ref, f32[96,768]{1,0:T(8,128)S(1)} %copy-done.1, f32[96,768]{1,0:T(8,128)} %get-tuple-element.53.came_ref), custom_call_target="tpu_custom_call" | custom-call | tf_op jit(solution)/shard_map/bond/pallas_call | solution.py:68
  33.0 20.0 %all_to_all.15 = f32[16,96,128]{2,1,0:T(8,128)S(1)} all-to-all(f32[16,96,128]{2,1,0:T(8,128)S(1)} %bond.1), channel_id=1, replica_groups=mesh['y'=4,'zl'=4,'x'=4,'zh'=4,'core'=2] {'y','x'}, dimensions={0} | all-to-all | bytes 1572864 | tf_op jit(solution)/shard_map/all_to_all | solution.py:152
  53.1 0.0 copy-start
  53.2 8.2 %all_to_all.16 = f32[4,96,128]{2,1,0:T(8,128)S(1)} all-to-all(f32[4,96,128]{2,1,0:T(8,128)S(1)} %broadcast_in_dim.2), channel_id=1, replica_groups=mesh['y'=4,'zl'=4,'x'=4,'zh'=4,'core'=2] {'zl'}, dimensions={0} | all-to-all | bytes 393216 | tf_op jit(solution)/shard_map/all_to_all | solution.py:155
  61.3 1.9 %collective-permute-start.22 = (f32[96,128]{1,0:T(8,128)S(1)}, f32[96,128]{1,0:T(8,128)S(1)}, u32[]{:S(2)}, u32[]{:S(2)}) collective-permute-start(f32[96,128]{1,0:T(8,128)S(1)} %reduce_sum.28), channel_id=1, source_target_pairs={{0,38},{1,39},{2,198},{3,199},{4,258},{5,259},{6,482},{7,483},{8,4... | collective-permute-start | bytes 147464 | tf_op jit(solution)/shard_map/ppermute | solution.py:156
  63.3 5.3 %collective-permute-done.22.block_ref = f32[96,128]{1,0:T(8,128)S(1)} collective-permute-done((f32[96,128]{1,0:T(8,128)S(1)}, f32[96,128]{1,0:T(8,128)S(1)}, u32[]{:S(2)}, u32[]{:S(2)}) %collective-permute-start.22) | collective-permute-done | bytes 49184 | tf_op jit(solution)/shard_map/ppermute | solution.py:156
  68.6 6.6 %collective-permute-start.23 = (f32[96,128]{1,0:T(8,128)S(1)}, f32[96,128]{1,0:T(8,128)S(1)}, u32[]{:S(2)}, u32[]{:S(2)}) collective-permute-start(f32[96,128]{1,0:T(8,128)S(1)} %collective-permute-done.22.block_ref), channel_id=1, source_target_pairs={{0,1},{1,0},{2,3},{3,2},{4,5},{5,4},{6,7},{7,6},{8,9},{9,8},{10,11... | collective-permute-start | bytes 147464 | tf_op jit(solution)/shard_map/ppermute | solution.py:107
  75.2 0.0 copy-done
  75.2 0.4 shard_map.37.sum_ref
  75.5 0.5 collective-permute-done.23.block_ref
  76.0 0.4 shard_map.38
  76.4 24.0 %all_to_all.17.shares_ref = f32[64,2,768]{2,1,0:T(2,128)S(1)} all-to-all(f32[64,2,768]{2,1,0:T(2,128)S(1)} %shard_map.38), channel_id=1, replica_groups=mesh['y'=4,'zl'=4,'x'=4,'zh'=4,'core'=2] {'y','zl','x'}, dimensions={0} | all-to-all | bytes 786432 | tf_op jit(solution)/shard_map/all_to_all | solution.py:161
  100.4 0.8 shard_map.39
  (5 shorter events, 0.1 us)
Async XLA Ops:
  0.7 1.0 copy-start.1
  1.7 9.4 %collective-permute-start.7 = (f32[96,128]{1,0:T(8,128)S(1)}, f32[96,128]{1,0:T(8,128)S(1)}, u32[]{:S(2)}, u32[]{:S(2)}) collective-permute-start(f32[96,128]{1,0:T(8,128)S(1)} %get-tuple-element.39), channel_id=1, source_target_pairs={{2,3},{3,2},{10,11},{11,10},{18,19},{19,18},{26,27},{27,26},{34,35... | collective-permute-start | bytes 147464 | tf_op jit(solution)/shard_map/cond/branch_1_fun/ppermute | solution.py:113
  2.3 28.6 %collective-permute-start.11 = (f32[96,768]{1,0:T(8,128)S(1)}, f32[96,768]{1,0:T(8,128)}, u32[]{:S(2)}, u32[]{:S(2)}) collective-permute-start(f32[96,768]{1,0:T(8,128)S(1)} %get-tuple-element.40), channel_id=1, source_target_pairs={{0,1},{1,0},{2,3},{3,2},{4,5},{5,4},{6,7},{7,6},{8,9},{9,8},{10,11... | collective-permute-start | bytes 884744 | tf_op jit(solution)/shard_map/cond/branch_1_fun/ppermute | solution.py:116
  11.1 2.7 %collective-permute-start.10 = (f32[96,128]{1,0:T(8,128)S(1)}, f32[96,128]{1,0:T(8,128)S(1)}, u32[]{:S(2)}, u32[]{:S(2)}) collective-permute-start(f32[96,128]{1,0:T(8,128)S(1)} %add.55), channel_id=1, source_target_pairs={{2,6},{3,7},{10,14},{11,15},{18,22},{19,23},{26,30},{27,31},{34,38... | collective-permute-start | bytes 147464 | tf_op jit(solution)/shard_map/cond/branch_1_fun/ppermute | solution.py:115
  11.8 2.0 %collective-permute-start.9 = (f32[96,128]{1,0:T(8,128)S(1)}, f32[96,128]{1,0:T(8,128)S(1)}, u32[]{:S(2)}, u32[]{:S(2)}) collective-permute-start(f32[96,128]{1,0:T(8,128)S(1)} %add.55), channel_id=1, source_target_pairs={{2,4},{3,5},{10,12},{11,13},{18,20},{19,21},{26,28},{27,29},{34,36... | collective-permute-start | bytes 147464 | tf_op jit(solution)/shard_map/cond/branch_1_fun/ppermute | solution.py:115
  12.5 18.5 %collective-permute-start.8 = (f32[96,128]{1,0:T(8,128)S(1)}, f32[96,128]{1,0:T(8,128)S(1)}, u32[]{:S(2)}, u32[]{:S(2)}) collective-permute-start(f32[96,128]{1,0:T(8,128)S(1)} %add.55), channel_id=1, source_target_pairs={{2,0},{3,1},{10,8},{11,9},{18,16},{19,17},{26,24},{27,25},{34,32},... | collective-permute-start | bytes 147464 | tf_op jit(solution)/shard_map/cond/branch_1_fun/ppermute | solution.py:115
  53.1 22.0 %copy-start = (f32[2,96,768]{2,1,0:T(8,128)S(1)}, f32[2,96,768]{2,1,0:T(8,128)}, u32[]{:S(2)}) copy-start(f32[2,96,768]{2,1,0:T(8,128)} %tensors_ref.3) | copy-start | bytes 1769476
  61.3 7.2 %collective-permute-start.22 = (f32[96,128]{1,0:T(8,128)S(1)}, f32[96,128]{1,0:T(8,128)S(1)}, u32[]{:S(2)}, u32[]{:S(2)}) collective-permute-start(f32[96,128]{1,0:T(8,128)S(1)} %reduce_sum.28), channel_id=1, source_target_pairs={{0,38},{1,39},{2,198},{3,199},{4,258},{5,259},{6,482},{7,483},{8,4... | collective-permute-start | bytes 147464 | tf_op jit(solution)/shard_map/ppermute | solution.py:156
  68.6 7.5 %collective-permute-start.23 = (f32[96,128]{1,0:T(8,128)S(1)}, f32[96,128]{1,0:T(8,128)S(1)}, u32[]{:S(2)}, u32[]{:S(2)}) collective-permute-start(f32[96,128]{1,0:T(8,128)S(1)} %collective-permute-done.22.block_ref), channel_id=1, source_target_pairs={{0,1},{1,0},{2,3},{3,2},{4,5},{5,4},{6,7},{7,6},{8,9},{9,8},{10,11... | collective-permute-start | bytes 147464 | tf_op jit(solution)/shard_map/ppermute | solution.py:107

commit v7 on v6

--- a/solution.py
+++ b/solution.py
@@ -100,19 +100,31 @@
     out_ref[...] = jnp.sum(shares_ref[...], axis=0)
 
 
-TARGETS = ((1, 3, 2), (0, 2, 3), (0, 1, 3), (0, 1, 2))
+CASES = (
+    ((0,), (((0, 1),), ((0, 3),), ((0, 2),))),
+    ((1,), (((1, 0),), ((1, 2),), ((1, 3),))),
+    ((2,), (((2, 0),), ((2, 1),), ((2, 3),))),
+    ((3,), (((3, 0),), ((3, 1),), ((3, 2),))),
+    ((0, 1), (((0, 1), (1, 0)), ((0, 3), (1, 2)), ((0, 2), (1, 3)))),
+    ((1, 2), (((1, 0), (2, 3)), ((1, 2), (2, 1)), ((2, 0), (1, 3)))),
+    ((2, 3), (((2, 0), (3, 1)), ((3, 0), (2, 1)), ((2, 3), (3, 2)))),
+)
 
 
 def swap(values):
     return lax.ppermute(values, "core", [(0, 1), (1, 0)])
 
 
-def from_cube(owner):
+def from_owners(case):
+    owners, permutes = CASES[case]
+
     def spread(kept, sent, environment):
-        pair = [(2 * owner, 2 * owner + 1), (2 * owner + 1, 2 * owner)]
-        half = kept + lax.ppermute(sent, COL, pair)
-        held = jnp.where(lax.axis_index("zh") == owner, half, jnp.zeros_like(half))
-        parts = [lax.ppermute(half, "zh", [(owner, to)]) for to in TARGETS[owner]]
+        inside = [(2 * zh + core, 2 * zh + 1 - core) for zh in owners for core in range(2)]
+        half = kept + lax.ppermute(sent, COL, inside)
+        cube = lax.axis_index("zh")
+        owned = (cube >= owners[0]) & (cube <= owners[-1])
+        held = jnp.where(owned, half, jnp.zeros_like(half))
+        parts = [lax.ppermute(half, "zh", pairs) for pairs in permutes]
         came = lax.ppermute(environment, "core", [(0, 1), (1, 0)])
         for part in parts:
             held = held + part
@@ -121,18 +133,12 @@
     return spread
 
 
-def from_all_cubes(kept, sent, environment):
-    half = kept + swap(sent)
-    return lax.all_gather(half, "zh").sum(axis=0), swap(environment)
-
-
 def panel_of(kept, sent, environment, offset):
     cols = 2 * environment.shape[1]
     first = offset // cols
     last = (offset + PANEL - 1) // cols
-    case = jnp.where(first == last, first, 4)
-    branches = [from_cube(zh) for zh in range(4)] + [from_all_cubes]
-    return lax.switch(case, branches, kept, sent, environment)
+    case = jnp.where(first == last, first, 4 + first)
+    return lax.switch(case, [from_owners(n) for n in range(len(CASES))], kept, sent, environment)
 
 
 def shards(environment, site_tensors, panel_offset):

time: 102 us -> 102 us (level)
  no operation moved by 1% of the time
where the time goes in v7:
time: 102 us; the launch traced here: 101 us
  blocking collectives  52.1 us (51%)
  waiting for transfers between devices  23 us (23%)
  starting transfers between devices  20.5 us (20%)
  Pallas kernels  3.57 us (4%)
    all_to_all x1, blocking collectives, shards(): shares = lax.all_to_all(total, ROW, 0, 0, tiled=True)  24 us
    all_to_all x1, blocking collectives, shards(): pieces = lax.all_to_all(pieces, ('y', 'x'), 0, 0, tiled=True)  20 us
    ppermute x3, waiting for transfers between devices, spread(): parts = [lax.ppermute(half, 'zh', pairs) for pairs in permutes]  17.2 us
    ppermute x1, starting transfers between devices, spread(): came = lax.ppermute(environment, 'core', [(0, 1), (1, 0)])  8.75 us
    all_to_all x1, blocking collectives, shards(): piece = lax.all_to_all(copies, 'zl', 0, 0, tiled=True).sum(axis=0)  8.15 us
    ppermute x1, starting transfers between devices, swap(): return lax.ppermute(values, 'core', [(0, 1), (1, 0)])  6.59 us
    ppermute x1, waiting for transfers between devices, shards(): mine = lax.ppermute(piece, ALL, deliveries())  5.31 us
    ppermute x3, starting transfers between devices, spread(): parts = [lax.ppermute(half, 'zh', pairs) for pairs in permutes]  2.62 us
  transfers between devices with their start and end apart: 7, of which 3 were waited for; matrix products, arithmetic and copies ran while one was open for 0% of the time, Pallas kernels for 0%

profile of v7, /device:TPU:1, one launch (start us, length us, event | category | flops | bytes accessed | tf_op | source)
XLA Modules:
  0.0 101.2 jit_solution(13140044958753765958)
XLA Ops:
  0.7 0.0 copy-start.1
  0.7 0.1 fusion.1
  0.8 0.8 copy-done.1
  1.7 29.3 %conditional.1 = (f32[96,128]{1,0:T(8,128)S(1)}, f32[96,768]{1,0:T(8,128)}) conditional(s32[]{:T(128)} %clamp.3, (f32[96,128]{1,0:T(8,128)S(1)}, f32[96,128]{1,0:T(8,128)S(1)}, f32[96,768]{1,0:T(8,128)S(1)}) %tuple.42, (f32[96,128]{1,0:T(8,128)S(1)}, f32[96,128]{1,0:T(8,128)S(1)}, f32[96,768]{1,0:T(8,128)S(1)}) %tuple.43, ...), branch_computations={%region_0.1_spmd, %region_1.2_spmd, %region_2.3_spmd, %region_3.4_... | conditional | flops 61446 | bytes 2359566 | solution.py:141
  1.7 0.7 collective-permute-start.5
  2.3 8.7 %collective-permute-start.9 = (f32[96,768]{1,0:T(8,128)S(1)}, f32[96,768]{1,0:T(8,128)}, u32[]{:S(2)}, u32[]{:S(2)}) collective-permute-start(f32[96,768]{1,0:T(8,128)S(1)} %get-tuple-element.52), channel_id=1, source_target_pairs={{0,1},{1,0},{2,3},{3,2},{4,5},{5,4},{6,7},{7,6},{8,9},{9,8},{10,11... | collective-permute-start | bytes 884744 | tf_op jit(solution)/shard_map/cond/branch_1_fun/ppermute | solution.py:128
  11.1 0.0 collective-permute-done.5
  11.1 0.7 collective-permute-start.8
  11.8 0.7 collective-permute-start.7
  12.5 1.3 %collective-permute-start.6 = (f32[96,128]{1,0:T(8,128)S(1)}, f32[96,128]{1,0:T(8,128)S(1)}, u32[]{:S(2)}, u32[]{:S(2)}) collective-permute-start(f32[96,128]{1,0:T(8,128)S(1)} %add.77), channel_id=1, source_target_pairs={{2,0},{3,1},{10,8},{11,9},{18,16},{19,17},{26,24},{27,25},{34,32},... | collective-permute-start | bytes 147464 | tf_op jit(solution)/shard_map/cond/branch_1_fun/ppermute | solution.py:127
  13.8 0.0 collective-permute-done.8
  13.8 0.0 collective-permute-done.7
  13.8 17.2 %collective-permute-done.6 = f32[96,128]{1,0:T(8,128)S(1)} collective-permute-done((f32[96,128]{1,0:T(8,128)S(1)}, f32[96,128]{1,0:T(8,128)S(1)}, u32[]{:S(2)}, u32[]{:S(2)}) %collective-permute-start.6) | collective-permute-done | bytes 49184 | tf_op jit(solution)/shard_map/cond/branch_1_fun/ppermute | solution.py:127
  31.0 0.0 collective-permute-done.9
  31.0 2.1 %bond.1 = f32[16,96,128]{2,1,0:T(8,128)S(1)} custom-call(f32[96,128]{1,0:T(8,128)S(1)} %get-tuple-element.70.panel_ref, f32[96,768]{1,0:T(8,128)S(1)} %copy-done.1, f32[96,768]{1,0:T(8,128)} %get-tuple-element.71.came_ref), custom_call_target="tpu_custom_call" | custom-call | tf_op jit(solution)/shard_map/bond/pallas_call | solution.py:68
  33.1 20.0 %all_to_all.15 = f32[16,96,128]{2,1,0:T(8,128)S(1)} all-to-all(f32[16,96,128]{2,1,0:T(8,128)S(1)} %bond.1), channel_id=1, replica_groups=mesh['y'=4,'zl'=4,'x'=4,'zh'=4,'core'=2] {'y','x'}, dimensions={0} | all-to-all | bytes 1572864 | tf_op jit(solution)/shard_map/all_to_all | solution.py:158
  53.1 0.0 copy-start
  53.2 8.2 %all_to_all.16 = f32[4,96,128]{2,1,0:T(8,128)S(1)} all-to-all(f32[4,96,128]{2,1,0:T(8,128)S(1)} %broadcast_in_dim.2), channel_id=1, replica_groups=mesh['y'=4,'zl'=4,'x'=4,'zh'=4,'core'=2] {'zl'}, dimensions={0} | all-to-all | bytes 393216 | tf_op jit(solution)/shard_map/all_to_all | solution.py:161
  61.3 1.9 %collective-permute-start.35 = (f32[96,128]{1,0:T(8,128)S(1)}, f32[96,128]{1,0:T(8,128)S(1)}, u32[]{:S(2)}, u32[]{:S(2)}) collective-permute-start(f32[96,128]{1,0:T(8,128)S(1)} %reduce_sum.19), channel_id=1, source_target_pairs={{0,38},{1,39},{2,198},{3,199},{4,258},{5,259},{6,482},{7,483},{8,4... | collective-permute-start | bytes 147464 | tf_op jit(solution)/shard_map/ppermute | solution.py:162
  63.3 5.3 %collective-permute-done.35.block_ref = f32[96,128]{1,0:T(8,128)S(1)} collective-permute-done((f32[96,128]{1,0:T(8,128)S(1)}, f32[96,128]{1,0:T(8,128)S(1)}, u32[]{:S(2)}, u32[]{:S(2)}) %collective-permute-start.35) | collective-permute-done | bytes 49184 | tf_op jit(solution)/shard_map/ppermute | solution.py:162
  68.6 6.6 %collective-permute-start.36 = (f32[96,128]{1,0:T(8,128)S(1)}, f32[96,128]{1,0:T(8,128)S(1)}, u32[]{:S(2)}, u32[]{:S(2)}) collective-permute-start(f32[96,128]{1,0:T(8,128)S(1)} %collective-permute-done.35.block_ref), channel_id=1, source_target_pairs={{0,1},{1,0},{2,3},{3,2},{4,5},{5,4},{6,7},{7,6},{8,9},{9,8},{10,11... | collective-permute-start | bytes 147464 | tf_op jit(solution)/shard_map/ppermute | solution.py:115
  75.2 0.0 copy-done
  75.2 0.4 shard_map.37.sum_ref
  75.5 0.5 collective-permute-done.36.block_ref
  76.0 0.4 shard_map.38
  76.4 24.0 %all_to_all.17.shares_ref = f32[64,2,768]{2,1,0:T(2,128)S(1)} all-to-all(f32[64,2,768]{2,1,0:T(2,128)S(1)} %shard_map.38), channel_id=1, replica_groups=mesh['y'=4,'zl'=4,'x'=4,'zh'=4,'core'=2] {'y','zl','x'}, dimensions={0} | all-to-all | bytes 786432 | tf_op jit(solution)/shard_map/all_to_all | solution.py:167
  100.4 0.8 shard_map.39
  (5 shorter events, 0.1 us)
Async XLA Ops:
  0.7 1.0 copy-start.1
  1.7 9.4 %collective-permute-start.5 = (f32[96,128]{1,0:T(8,128)S(1)}, f32[96,128]{1,0:T(8,128)S(1)}, u32[]{:S(2)}, u32[]{:S(2)}) collective-permute-start(f32[96,128]{1,0:T(8,128)S(1)} %get-tuple-element.51), channel_id=1, source_target_pairs={{2,3},{3,2},{10,11},{11,10},{18,19},{19,18},{26,27},{27,26},{34,35... | collective-permute-start | bytes 147464 | tf_op jit(solution)/shard_map/cond/branch_1_fun/ppermute | solution.py:123
  2.3 28.6 %collective-permute-start.9 = (f32[96,768]{1,0:T(8,128)S(1)}, f32[96,768]{1,0:T(8,128)}, u32[]{:S(2)}, u32[]{:S(2)}) collective-permute-start(f32[96,768]{1,0:T(8,128)S(1)} %get-tuple-element.52), channel_id=1, source_target_pairs={{0,1},{1,0},{2,3},{3,2},{4,5},{5,4},{6,7},{7,6},{8,9},{9,8},{10,11... | collective-permute-start | bytes 884744 | tf_op jit(solution)/shard_map/cond/branch_1_fun/ppermute | solution.py:128
  11.1 2.7 %collective-permute-start.8 = (f32[96,128]{1,0:T(8,128)S(1)}, f32[96,128]{1,0:T(8,128)S(1)}, u32[]{:S(2)}, u32[]{:S(2)}) collective-permute-start(f32[96,128]{1,0:T(8,128)S(1)} %add.77), channel_id=1, source_target_pairs={{2,6},{3,7},{10,14},{11,15},{18,22},{19,23},{26,30},{27,31},{34,38... | collective-permute-start | bytes 147464 | tf_op jit(solution)/shard_map/cond/branch_1_fun/ppermute | solution.py:127
  11.8 2.0 %collective-permute-start.7 = (f32[96,128]{1,0:T(8,128)S(1)}, f32[96,128]{1,0:T(8,128)S(1)}, u32[]{:S(2)}, u32[]{:S(2)}) collective-permute-start(f32[96,128]{1,0:T(8,128)S(1)} %add.77), channel_id=1, source_target_pairs={{2,4},{3,5},{10,12},{11,13},{18,20},{19,21},{26,28},{27,29},{34,36... | collective-permute-start | bytes 147464 | tf_op jit(solution)/shard_map/cond/branch_1_fun/ppermute | solution.py:127
  12.5 18.5 %collective-permute-start.6 = (f32[96,128]{1,0:T(8,128)S(1)}, f32[96,128]{1,0:T(8,128)S(1)}, u32[]{:S(2)}, u32[]{:S(2)}) collective-permute-start(f32[96,128]{1,0:T(8,128)S(1)} %add.77), channel_id=1, source_target_pairs={{2,0},{3,1},{10,8},{11,9},{18,16},{19,17},{26,24},{27,25},{34,32},... | collective-permute-start | bytes 147464 | tf_op jit(solution)/shard_map/cond/branch_1_fun/ppermute | solution.py:127
  53.1 22.0 %copy-start = (f32[2,96,768]{2,1,0:T(8,128)S(1)}, f32[2,96,768]{2,1,0:T(8,128)}, u32[]{:S(2)}) copy-start(f32[2,96,768]{2,1,0:T(8,128)} %tensors_ref.3) | copy-start | bytes 1769476
  61.3 7.2 %collective-permute-start.35 = (f32[96,128]{1,0:T(8,128)S(1)}, f32[96,128]{1,0:T(8,128)S(1)}, u32[]{:S(2)}, u32[]{:S(2)}) collective-permute-start(f32[96,128]{1,0:T(8,128)S(1)} %reduce_sum.19), channel_id=1, source_target_pairs={{0,38},{1,39},{2,198},{3,199},{4,258},{5,259},{6,482},{7,483},{8,4... | collective-permute-start | bytes 147464 | tf_op jit(solution)/shard_map/ppermute | solution.py:162
  68.6 7.5 %collective-permute-start.36 = (f32[96,128]{1,0:T(8,128)S(1)}, f32[96,128]{1,0:T(8,128)S(1)}, u32[]{:S(2)}, u32[]{:S(2)}) collective-permute-start(f32[96,128]{1,0:T(8,128)S(1)} %collective-permute-done.35.block_ref), channel_id=1, source_target_pairs={{0,1},{1,0},{2,3},{3,2},{4,5},{5,4},{6,7},{7,6},{8,9},{9,8},{10,11... | collective-permute-start | bytes 147464 | tf_op jit(solution)/shard_map/ppermute | solution.py:115
